TPU v7x, 32 devices: a whole 2x2x4 slice. The times are simulated.
32 devices in a mesh: dp: 8 (over y, x, core), tensor: 4 (over z).
Axes of the slice: x: 2, y: 2, z: 4, core: 2. Of those that a mesh axis runs over, the one named last changes fastest.
Arguments:
- image: bfloat16 [8, 1024, 1536], P('dp'), may hold values from -6 to 6
- text: bfloat16 [8, 154, 1536], P('dp'), may hold values from -6 to 6
- pooled: bfloat16 [8, 1536], P('dp', 'tensor'), may hold values from -6 to 6
- timestep: int32 [8], P('dp'), may hold values from 0 to 999
- grad_image: bfloat16 [8, 1024, 1536], P('dp'), may hold values from -6 to 6
- grad_text: bfloat16 [8, 154, 1536], P('dp'), may hold values from -6 to 6
- ada_weight: bfloat16 [2, 1536, 9216], P(None, 'tensor', 'dp'), may hold values from -0.15625 to 0.15625
- ada_bias: bfloat16 [2, 9216], replicated, may hold values from -2.390625 to 2.390625
- qkv_weight: bfloat16 [2, 1536, 3, 1536], P(None, 'dp', None, 'tensor'), may hold values from -0.102062073 to 0.102062073
- qv_bias: bfloat16 [2, 2, 1536], P(None, None, 'tensor'), may hold values from -3 to 3
- out_weight: bfloat16 [2, 1536, 1536], P(None, 'tensor', 'dp'), may hold values from -1.25 to 1.25
- out_bias: bfloat16 [2, 1536], replicated, may hold values from -2.390625 to 2.390625
- mlp_in_weight: bfloat16 [2, 1536, 6144], P(None, 'dp', 'tensor'), may hold values from -0.15625 to 0.15625
- mlp_in_bias: bfloat16 [2, 6144], P(None, 'tensor'), may hold values from -3 to 3
- mlp_out_weight: bfloat16 [2, 6144, 1536], P(None, 'tensor', 'dp'), may hold values from -0.078125 to 0.078125
- mlp_out_bias: bfloat16 [2, 1536], replicated, may hold values from -2.390625 to 2.390625
Outputs:
- block_image: bfloat16 [8, 1024, 1536], P('dp')
- block_text: bfloat16 [8, 154, 1536], P('dp')
- image_grad: float32 [8, 1024, 1536], P('dp')
- text_grad: float32 [8, 154, 1536], P('dp')
- pooled_grad: float32 [8, 1536], P('dp', 'tensor')
- ada_weight_grad: float32 [2, 1536, 9216], P(None, 'tensor', 'dp')
- ada_bias_grad: float32 [2, 9216], replicated
- qkv_weight_grad: float32 [2, 1536, 3, 1536], P(None, 'dp', None, 'tensor')
- qv_bias_grad: float32 [2, 2, 1536], P(None, None, 'tensor')
- out_weight_grad: float32 [2, 1536, 1536], P(None, 'tensor', 'dp')
- out_bias_grad: float32 [2, 1536], replicated
- mlp_in_weight_grad: float32 [2, 1536, 6144], P(None, 'dp', 'tensor')
- mlp_in_bias_grad: float32 [2, 6144], P(None, 'tensor')
- mlp_out_weight_grad: float32 [2, 6144, 1536], P(None, 'tensor', 'dp')
- mlp_out_bias_grad: float32 [2, 1536], replicated
All inputs are finite; a program needn't handle non-finite values.
Results may differ from a plain program's by a relative error of at most 0.02.
Values may be sent and summed in bfloat16 or wider, within the bound.
A program may use at most 256 MiB of HBM per device.

v0:
```python
import math

import jax
import jax.numpy as jnp
from jax import lax
from jax.sharding import PartitionSpec as P

D = 1536
HEAD_DIM = 64


def layer_norm(inputs):
    center = inputs - jnp.mean(inputs, axis=-1, keepdims=True)
    spread = jnp.mean(center * center, axis=-1, keepdims=True)
    return center * lax.rsqrt(spread + 1e-06)


def modulate(inputs, shift_by, scale_by):
    return layer_norm(inputs) * (1.0 + scale_by) + shift_by


def gelu_tanh(inputs):
    return jax.nn.gelu(inputs, approximate=True)


def time_embed(time_steps, first_col, width_count):
    feature_idx = first_col + jnp.arange(width_count, dtype=jnp.int32)
    half_width = D // 2
    frequency = jnp.exp(
        -math.log(10000.0) * (feature_idx % half_width).astype(jnp.float32) / half_width
    )
    phase_arg = time_steps.astype(jnp.float32)[:, None] * frequency[None, :]
    return jnp.where(feature_idx[None, :] < half_width, jnp.cos(phase_arg), jnp.sin(phase_arg))


def split_heads(inputs):
    return inputs.reshape(inputs.shape[0], inputs.shape[1] // HEAD_DIM, HEAD_DIM)


def attend_block(queries, key_rows, value_rows):
    q_heads = split_heads(queries)
    k_heads = split_heads(key_rows)
    v_heads = split_heads(value_rows)
    scores = jnp.einsum(
        "qhd,khd->hqk", q_heads, k_heads, preferred_element_type=jnp.float32
    ) * HEAD_DIM ** (-0.5)
    row_max = jnp.max(scores, axis=-1, keepdims=True)
    exp_scores = jnp.exp(scores - row_max)
    row_sum = jnp.sum(exp_scores, axis=-1, keepdims=True)
    weights = (exp_scores / row_sum).astype(jnp.bfloat16)
    mixed_out = jnp.einsum("hqk,khd->qhd", weights, v_heads, preferred_element_type=jnp.float32)
    logsum = (row_max + jnp.log(row_sum))[..., 0]
    return (mixed_out.reshape(queries.shape).astype(jnp.bfloat16), logsum)


def attend_sequence(sequence):
    queries, key_rows, value_rows = sequence
    half_rows = queries.shape[0] // 2
    blocks = queries.reshape(2, half_rows, queries.shape[1])
    mixed_out, logsum = lax.map(
        lambda block_in: attend_block(block_in, key_rows, value_rows), blocks
    )
    return (mixed_out.reshape(queries.shape), logsum)


def attend_block_back(queries, key_rows, value_rows, grad_rows, logsum):
    q_heads = split_heads(queries)
    k_heads = split_heads(key_rows)
    v_heads = split_heads(value_rows)
    g_heads = split_heads(grad_rows)
    scale_by = HEAD_DIM ** (-0.5)
    scores = (
        jnp.einsum("qhd,khd->hqk", q_heads, k_heads, preferred_element_type=jnp.float32) * scale_by
    )
    prob_rows = jnp.exp(scores - logsum[..., None])
    grad_prob = jnp.einsum("qhd,khd->hqk", g_heads, v_heads, preferred_element_type=jnp.float32)
    row_delta = jnp.sum(grad_prob * prob_rows, axis=-1, keepdims=True)
    grad_score = (prob_rows * (grad_prob - row_delta)).astype(jnp.bfloat16)
    grad_query = (
        jnp.einsum("hqk,khd->qhd", grad_score, k_heads, preferred_element_type=jnp.float32)
        * scale_by
    )
    grad_key = (
        jnp.einsum("hqk,qhd->khd", grad_score, q_heads, preferred_element_type=jnp.float32)
        * scale_by
    )
    grad_value = jnp.einsum(
        "hqk,qhd->khd", prob_rows.astype(jnp.bfloat16), g_heads, preferred_element_type=jnp.float32
    )
    return (
        grad_query.reshape(queries.shape),
        grad_key.reshape(key_rows.shape),
        grad_value.reshape(value_rows.shape),
    )


def attend_sequence_back(sequence):
    queries, key_rows, value_rows, grad_rows, logsum = sequence
    half_rows = queries.shape[0] // 2
    query_blocks = queries.reshape(2, half_rows, queries.shape[1])
    grad_blocks = grad_rows.reshape(2, half_rows, grad_rows.shape[1])

    def block_step(running, block_in):
        query_part, grad_part, logsum_part = block_in
        grad_query, grad_key, grad_value = attend_block_back(
            query_part, key_rows, value_rows, grad_part, logsum_part
        )
        return ((running[0] + grad_key, running[1] + grad_value), grad_query)

    zero_rows = jnp.zeros(key_rows.shape, jnp.float32)
    (grad_key, grad_value), grad_query = lax.scan(
        block_step, (zero_rows, zero_rows), (query_blocks, grad_blocks, logsum)
    )
    return (
        grad_query.reshape(queries.shape).astype(jnp.bfloat16),
        grad_key.astype(jnp.bfloat16),
        grad_value.astype(jnp.bfloat16),
    )


def shards(
    image,
    text,
    pooled,
    timestep,
    grad_image,
    grad_text,
    ada_weight,
    ada_bias,
    qkv_weight,
    qv_bias,
    out_weight,
    out_bias,
    mlp_in_weight,
    mlp_in_bias,
    mlp_out_weight,
    mlp_out_bias,
):
    width_local = pooled.shape[1]
    first_col = lax.axis_index("tensor") * width_local
    condition = pooled.astype(jnp.float32) + time_embed(timestep, first_col, width_local)
    cond_act, silu_pull = jax.vjp(jax.nn.silu, condition)
    cond_low = cond_act.astype(jnp.bfloat16)
    ada_full, query_key_value_whole, out_full = (
        lax.all_gather(ada_weight, "dp", axis=2, tiled=True),
        lax.all_gather(qkv_weight, "dp", axis=1, tiled=True),
        lax.all_gather(out_weight, "dp", axis=2, tiled=True),
    )
    mod_part = jnp.einsum("sc,nce->nse", cond_low, ada_full, preferred_element_type=jnp.float32)
    modul = lax.psum(mod_part, "tensor") + ada_bias.astype(jnp.float32)[:, None, :]
    seq_count = modul.shape[1]
    modul = modul.reshape(2, seq_count, 6, 1, D)
    out_bias_f = out_bias.astype(jnp.float32)
    in_bias_f = mlp_in_bias.astype(jnp.float32)
    last_bias_f = mlp_out_bias.astype(jnp.float32)
    pair_bias = qv_bias.astype(jnp.float32)
    streams = (image.astype(jnp.float32), text.astype(jnp.float32))
    cotangents = (grad_image.astype(jnp.float32), grad_text.astype(jnp.float32))
    first_pulls, lowered_input_list, query_list, key_list, value_list = ([], [], [], [], [])
    for modality_branch in range(2):
        normed, first_pull = jax.vjp(
            modulate,
            streams[modality_branch],
            modul[modality_branch, :, 0],
            modul[modality_branch, :, 1],
        )
        lowered_input = normed.astype(jnp.bfloat16)
        projected = jnp.einsum(
            "hbr,rfu->hbfu",
            lowered_input,
            query_key_value_whole[modality_branch],
            preferred_element_type=jnp.float32,
        )
        query_list.append((projected[:, :, 0] + pair_bias[modality_branch, 0]).astype(jnp.bfloat16))
        key_list.append(projected[:, :, 1].astype(jnp.bfloat16))
        value_list.append((projected[:, :, 2] + pair_bias[modality_branch, 1]).astype(jnp.bfloat16))
        first_pulls.append(first_pull)
        lowered_input_list.append(lowered_input)
    joint_q = jnp.concatenate(query_list, axis=1)
    joint_k = jnp.concatenate(key_list, axis=1)
    joint_v = jnp.concatenate(value_list, axis=1)
    attn_mix, logsum = lax.map(attend_sequence, (joint_q, joint_k, joint_v))
    split_at = image.shape[1]
    mix_parts = (attn_mix[:, :split_at], attn_mix[:, split_at:])
    attn_terms = tuple(
        (
            jnp.einsum(
                "acn,nz->acz",
                mix_parts[modality_branch],
                out_full[modality_branch],
                preferred_element_type=jnp.float32,
            )
            for modality_branch in range(2)
        )
    )
    input_weight_whole, output_weight_whole = (
        lax.all_gather(mlp_in_weight, "dp", axis=1, tiled=True),
        lax.all_gather(mlp_out_weight, "dp", axis=2, tiled=True),
    )
    branches, resids, second_pulls, lowered_middle_list = ([], [], [], [])
    attn_sum = (
        lax.psum(attn_terms[0].astype(jnp.bfloat16), "tensor").astype(jnp.float32),
        lax.psum(attn_terms[1].astype(jnp.bfloat16), "tensor").astype(jnp.float32),
    )
    for modality_branch in range(2):
        branch = attn_sum[modality_branch] + out_bias_f[modality_branch]
        resid = streams[modality_branch] + modul[modality_branch, :, 2] * branch
        normed_mid, second_pull = jax.vjp(
            modulate, resid, modul[modality_branch, :, 3], modul[modality_branch, :, 4]
        )
        lowered_middle_list.append(normed_mid.astype(jnp.bfloat16))
        branches.append(branch)
        resids.append(resid)
        second_pulls.append(second_pull)
    gelu_pulls, activation_lowered_list, mlp_terms = ([], [], [])
    for modality_branch in range(2):
        upper = (
            jnp.einsum(
                "wic,ch->wih",
                lowered_middle_list[modality_branch],
                input_weight_whole[modality_branch],
                preferred_element_type=jnp.float32,
            )
            + in_bias_f[modality_branch]
        )
        act_value, gelu_pull = jax.vjp(gelu_tanh, upper)
        activation_lowered = act_value.astype(jnp.bfloat16)
        mlp_terms.append(
            jnp.einsum(
                "qjt,tx->qjx",
                activation_lowered,
                output_weight_whole[modality_branch],
                preferred_element_type=jnp.float32,
            )
        )
        gelu_pulls.append(gelu_pull)
        activation_lowered_list.append(activation_lowered)
    mlp_sum = (
        lax.psum(mlp_terms[0].astype(jnp.bfloat16), "tensor").astype(jnp.float32),
        lax.psum(mlp_terms[1].astype(jnp.bfloat16), "tensor").astype(jnp.float32),
    )
    block_out, gate2_grads = ([], [])
    for modality_branch in range(2):
        second_branch = mlp_sum[modality_branch] + last_bias_f[modality_branch]
        block_out.append(
            (resids[modality_branch] + modul[modality_branch, :, 5] * second_branch).astype(
                jnp.bfloat16
            )
        )
        gate2_grads.append(jnp.sum(cotangents[modality_branch] * second_branch, axis=1))
    bias2_grads, w_out_grads, bias1_grads, w_in_grads, mid_terms = ([], [], [], [], [])
    for modality_branch in range(2):
        cot_rows = cotangents[modality_branch]
        d_mlp = modul[modality_branch, :, 5] * cot_rows
        bias2_grads.append(jnp.sum(d_mlp, axis=(0, 1)))
        mlp_gradient_lowered = d_mlp.astype(jnp.bfloat16)
        w_out_grads.append(
            jnp.einsum(
                "equ,eqo->uo",
                activation_lowered_list[modality_branch],
                mlp_gradient_lowered,
                preferred_element_type=jnp.float32,
            )
        )
        d_act = jnp.einsum(
            "kbp,gp->kbg",
            mlp_gradient_lowered,
            output_weight_whole[modality_branch],
            preferred_element_type=jnp.float32,
        )
        (d_upper,) = gelu_pulls[modality_branch](d_act)
        upper_gradient_lowered = d_upper.astype(jnp.bfloat16)
        bias1_grads.append(jnp.sum(upper_gradient_lowered.astype(jnp.float32), axis=(0, 1)))
        w_in_grads.append(
            jnp.einsum(
                "typ,tyq->pq",
                lowered_middle_list[modality_branch],
                upper_gradient_lowered,
                preferred_element_type=jnp.float32,
            )
        )
        mid_terms.append(
            jnp.einsum(
                "viq,pq->vip",
                upper_gradient_lowered,
                input_weight_whole[modality_branch],
                preferred_element_type=jnp.float32,
            )
        )
    w_in_grad_all = jnp.stack(w_in_grads)
    w_out_grad_all = jnp.stack(w_out_grads)
    w_in_shard, w_out_shard = (
        lax.psum_scatter(
            w_in_grad_all.astype(jnp.bfloat16), "dp", scatter_dimension=1, tiled=True
        ).astype(jnp.float32),
        lax.psum_scatter(
            w_out_grad_all.astype(jnp.bfloat16), "dp", scatter_dimension=2, tiled=True
        ).astype(jnp.float32),
    )
    d_resids, shift2_grads, scale2_grads, gate1_grads, outb_grads = ([], [], [], [], [])
    d_mid = (
        lax.psum(mid_terms[0].astype(jnp.bfloat16), "tensor").astype(jnp.float32),
        lax.psum(mid_terms[1].astype(jnp.bfloat16), "tensor").astype(jnp.float32),
    )
    d_attn_lows = []
    for modality_branch in range(2):
        d_resid, shift_two, scale_two = second_pulls[modality_branch](d_mid[modality_branch])
        d_resid = d_resid + cotangents[modality_branch]
        d_attn = modul[modality_branch, :, 2] * d_resid
        outb_grads.append(jnp.sum(d_attn, axis=(0, 1)))
        gate1_grads.append(jnp.sum(d_resid * branches[modality_branch], axis=1))
        d_attn_lows.append(d_attn.astype(jnp.bfloat16))
        d_resids.append(d_resid)
        shift2_grads.append(shift_two[:, 0])
        scale2_grads.append(scale_two[:, 0])
    out_grads, d_mix_list = ([], [])
    for modality_branch in range(2):
        out_grads.append(
            jnp.einsum(
                "kyb,kyt->bt",
                mix_parts[modality_branch],
                d_attn_lows[modality_branch],
                preferred_element_type=jnp.float32,
            )
        )
        d_mix_list.append(
            jnp.einsum(
                "xkm,am->xka",
                d_attn_lows[modality_branch],
                out_full[modality_branch],
                preferred_element_type=jnp.float32,
            ).astype(jnp.bfloat16)
        )
    d_mix_joint = jnp.concatenate(d_mix_list, axis=1)
    d_query, d_key, d_value = lax.map(
        attend_sequence_back, (joint_q, joint_k, joint_v, d_mix_joint, logsum)
    )
    qkv_grads, pair_grads, in_terms = ([], [], [])
    for modality_branch in range(2):
        rows_from = 0 if modality_branch == 0 else split_at
        rows_to = split_at if modality_branch == 0 else d_query.shape[1]
        projection_gradient = jnp.stack(
            [
                d_query[:, rows_from:rows_to],
                d_key[:, rows_from:rows_to],
                d_value[:, rows_from:rows_to],
            ],
            axis=2,
        )
        qkv_grads.append(
            jnp.einsum(
                "pjw,pjmb->wmb",
                lowered_input_list[modality_branch],
                projection_gradient,
                preferred_element_type=jnp.float32,
            )
        )
        pair_grads.append(
            jnp.stack(
                [
                    jnp.sum(projection_gradient[:, :, 0].astype(jnp.float32), axis=(0, 1)),
                    jnp.sum(projection_gradient[:, :, 2].astype(jnp.float32), axis=(0, 1)),
                ]
            )
        )
        in_terms.append(
            jnp.einsum(
                "rawn,uwn->rau",
                projection_gradient,
                query_key_value_whole[modality_branch],
                preferred_element_type=jnp.float32,
            )
        )
    d_in = (
        lax.psum(in_terms[0].astype(jnp.bfloat16), "tensor").astype(jnp.float32),
        lax.psum(in_terms[1].astype(jnp.bfloat16), "tensor").astype(jnp.float32),
    )
    token_grads, d_mods = ([], [])
    for modality_branch in range(2):
        d_tokens, shift_one, scale_one = first_pulls[modality_branch](d_in[modality_branch])
        token_grads.append(d_tokens + d_resids[modality_branch])
        d_mods.append(
            jnp.stack(
                [
                    shift_one[:, 0],
                    scale_one[:, 0],
                    gate1_grads[modality_branch],
                    shift2_grads[modality_branch],
                    scale2_grads[modality_branch],
                    gate2_grads[modality_branch],
                ],
                axis=1,
            )
        )
    ada_grads, adab_grads = ([], [])
    d_cond_act = jnp.zeros(cond_act.shape, jnp.float32)
    for modality_branch in range(2):
        d_mod_low = d_mods[modality_branch].reshape(seq_count, 6 * D).astype(jnp.bfloat16)
        adab_grads.append(jnp.sum(d_mod_low.astype(jnp.float32), axis=0))
        ada_grads.append(
            jnp.einsum("sc,se->ce", cond_low, d_mod_low, preferred_element_type=jnp.float32)
        )
        d_cond_act = d_cond_act + jnp.einsum(
            "se,ce->sc", d_mod_low, ada_full[modality_branch], preferred_element_type=jnp.float32
        )
    (pooled_grad,) = silu_pull(d_cond_act)
    ada_grad_all = jnp.stack(ada_grads)
    qkv_grad_all = jnp.stack(qkv_grads)
    out_grad_all = jnp.stack(out_grads)
    ada_shard, qkv_shard, out_shard = (
        lax.psum_scatter(
            ada_grad_all.astype(jnp.bfloat16), "dp", scatter_dimension=2, tiled=True
        ).astype(jnp.float32),
        lax.psum_scatter(
            qkv_grad_all.astype(jnp.bfloat16), "dp", scatter_dimension=1, tiled=True
        ).astype(jnp.float32),
        lax.psum_scatter(
            out_grad_all.astype(jnp.bfloat16), "dp", scatter_dimension=2, tiled=True
        ).astype(jnp.float32),
    )
    adab_sum, pair_sum, outb_sum, bias1_sum, bias2_sum = (
        lax.psum(jnp.stack(adab_grads).astype(jnp.bfloat16), "dp").astype(jnp.float32),
        lax.psum(jnp.stack(pair_grads).astype(jnp.bfloat16), "dp").astype(jnp.float32),
        lax.psum(jnp.stack(outb_grads).astype(jnp.bfloat16), "dp").astype(jnp.float32),
        lax.psum(jnp.stack(bias1_grads).astype(jnp.bfloat16), "dp").astype(jnp.float32),
        lax.psum(jnp.stack(bias2_grads).astype(jnp.bfloat16), "dp").astype(jnp.float32),
    )
    return (
        block_out[0],
        block_out[1],
        token_grads[0],
        token_grads[1],
        pooled_grad,
        ada_shard,
        adab_sum,
        qkv_shard,
        pair_sum,
        out_shard,
        outb_sum,
        w_in_shard,
        bias1_sum,
        w_out_shard,
        bias2_sum,
    )


def solution(mesh):
    return jax.shard_map(
        shards,
        mesh=mesh,
        in_specs=(
            P("dp", None, None),
            P("dp", None, None),
            P("dp", "tensor"),
            P("dp"),
            P("dp", None, None),
            P("dp", None, None),
            P(None, "tensor", "dp"),
            P(),
            P(None, "dp", None, "tensor"),
            P(None, None, "tensor"),
            P(None, "tensor", "dp"),
            P(),
            P(None, "dp", "tensor"),
            P(None, "tensor"),
            P(None, "tensor", "dp"),
            P(),
        ),
        out_specs=(
            P("dp", None, None),
            P("dp", None, None),
            P("dp", None, None),
            P("dp", None, None),
            P("dp", "tensor"),
            P(None, "tensor", "dp"),
            P(),
            P(None, "dp", None, "tensor"),
            P(None, None, "tensor"),
            P(None, "tensor", "dp"),
            P(),
            P(None, "dp", "tensor"),
            P(None, "tensor"),
            P(None, "tensor", "dp"),
            P(),
        ),
        check_vma=False,
    )
```

profile of v0, /device:TPU:0, one launch (start us, length us, event | category | flops | bytes accessed | tf_op | source)
XLA Modules:
  0.0 1525.8 jit_solution(10628418846768141458)
XLA Ops:
  10.0 81.2 %all-gather.6.cloned.1.call-done = bf16[2,384,9216]{2,1,0:T(8,128)(2,1)} async-done(((bf16[2,384,1152]{2,1,0:T(8,128)(2,1)}), bf16[2,384,9216]{2,1,0:T(8,128)(2,1)}) %all-gather.6.cloned.1.call-update) | async-done | bytes 14155792 | tf_op jit(solution)/shard_map/all_gather | solution.py:145
  105.0 28.3 %all-reduce.13.cloned.1.call-done = f32[2,1,9216]{2,0,1:T(2,128)} async-done(((f32[2,1,9216]{2,0,1:T(2,128)}), f32[2,1,9216]{2,0,1:T(2,128)}) %all-reduce.13.cloned.1.call-update) | async-done | bytes 73744 | tf_op jit(solution)/shard_map/psum | solution.py:150
  135.2 48.9 %all-gather.8.cloned.1.call-done = bf16[2,1536,3,384]{3,1,2,0:T(8,128)(2,1)} async-done(((bf16[2,192,3,384]{3,1,2,0:T(8,128)(2,1)}), bf16[2,1536,3,384]{3,1,2,0:T(8,128)(2,1)}) %all-gather.8.cloned.1.call-update) | async-done | bytes 7077904 | tf_op jit(solution)/shard_map/all_gather | solution.py:146
  202.9 57.0 %while.47 = (s32[]{:T(128)}, bf16[2,589,384]{2,1,0:T(8,128)(2,1)}, f32[2,6,589]{2,1,0:T(8,128)S(1)}, bf16[2,589,384]{1,2,0:T(8,128)(2,1)S(1)}, bf16[1178,384]{0,...) while((s32[]{:T(128)}, bf16[2,589,384]{2,1,0:T(8,128)(2,1)}, f32[2,6,589]{2,1,0:T(8,128)S(1)}, ...), condition=%wide.region_8.9_spmd, body=%wide.region_5.8_spmd.sunk | while | flops 1095105280 | bytes 55519368 | solution.py:60
  203.0 8.8 fusion.208
  211.8 8.9 fusion.209
  231.6 8.8 fusion.208
  240.4 8.8 fusion.209
  272.2 135.6 %all-reduce.21.cloned.1.call-done = (bf16[1,1024,1536]{2,1,0:T(8,128)(2,1)}, bf16[1,154,1536]{2,1,0:T(8,128)(2,1)}) async-done(((bf16[1,1024,1536]{2,1,0:T(8,128)(2,1)}, bf16[1,154,1536]{2,1,0:T(8,128)(2,1)}), (bf16[1,1024,1536]{2,1,0:T(8,128)(2,1)}, bf16[1,154,1536]{2,1,0:T(8,128)(2,1)})) %all-reduce.21.cloned.1.call-update) | async-done | bytes 3618832 | tf_op jit(solution)/shard_map/psum | solution.py:202
  415.9 51.3 %all-gather.12.cloned.1.call-done = bf16[2,1536,1536]{2,1,0:T(8,128)(2,1)} async-done(((bf16[2,192,1536]{2,1,0:T(8,128)(2,1)}), bf16[2,1536,1536]{2,1,0:T(8,128)(2,1)}) %all-gather.12.cloned.1.call-update) | async-done | bytes 9437200 | tf_op jit(solution)/shard_map/all_gather | solution.py:197
  467.2 10.8 fusion.41
  478.1 49.8 %all-gather.14.cloned.1.call-done = bf16[2,1536,1536]{1,2,0:T(8,128)(2,1)} async-done(((bf16[2,1536,192]{1,2,0:T(8,128)(2,1)}), bf16[2,1536,1536]{1,2,0:T(8,128)(2,1)}) %all-gather.14.cloned.1.call-update) | async-done | bytes 9437200 | tf_op jit(solution)/shard_map/all_gather | solution.py:198
  527.8 12.9 fusion.167
  558.8 10.7 fusion.54
  569.6 121.2 %all-reduce.19.cloned.1.call-done = (bf16[1,1024,1536]{2,1,0:T(8,128)(2,1)}, bf16[1,154,1536]{2,1,0:T(8,128)(2,1)}) async-done(((bf16[1,1024,1536]{2,1,0:T(8,128)(2,1)}, bf16[1,154,1536]{2,1,0:T(8,128)(2,1)}), (bf16[1,1024,1536]{2,1,0:T(8,128)(2,1)}, bf16[1,154,1536]{2,1,0:T(8,128)(2,1)})) %all-reduce.19.cloned.1.call-update) | async-done | bytes 3618832 | tf_op jit(solution)/shard_map/psum | solution.py:302
  716.2 95.6 %while.48 = (s32[]{:T(128)}, f32[1178,384]{0,1:T(8,128)}, f32[1178,384]{0,1:T(8,128)}, bf16[2,589,384]{1,2,0:T(8,128)(2,1)}, bf16[2,589,384]{1,2,0:T(8,128)(2,1)...) while((s32[]{:T(128)}, f32[1178,384]{0,1:T(8,128)}, ...), condition=%wide.region_25.26_spmd.clone, body=%wide.region_23.25_spmd.clone.sunk | while | flops 2700368384 | bytes 259955024 | solution.py:111
  728.4 15.4 %multiply_reduce_fusion.8 = (f32[6,589]{1,0:T(8,128)S(1)}, f32[6,589,1178]{2,1,0:T(8,128)}) fusion(f32[6,589,1178]{2,1,0:T(8,128)} %copy-done, bf16[589,6,64]{0,2,1:T(8,128)(2,1)} %bitcast.369, bf16[1178,6,64]{0,2,1:T(8,128)(2,1)} %bitcast.375), kind=kOutput, calls=%fused_computation.12.clone.1 | convolution fusion | flops 541193216 | bytes 34675608 | tf_op jit(solution)/shard_map/while/body/eval_jaxpr/while/body/eval_jaxpr/qhd,khd->hqk/dot_general | solution.py:76
  743.8 12.1 multiply_convert_fusion.12
  776.1 15.4 %multiply_reduce_fusion.8 = (f32[6,589]{1,0:T(8,128)S(1)}, f32[6,589,1178]{2,1,0:T(8,128)}) fusion(f32[6,589,1178]{2,1,0:T(8,128)} %copy-done, bf16[589,6,64]{0,2,1:T(8,128)(2,1)} %bitcast.369, bf16[1178,6,64]{0,2,1:T(8,128)(2,1)} %bitcast.375), kind=kOutput, calls=%fused_computation.12.clone.1 | convolution fusion | flops 541193216 | bytes 34675608 | tf_op jit(solution)/shard_map/while/body/eval_jaxpr/while/body/eval_jaxpr/qhd,khd->hqk/dot_general | solution.py:76
  791.5 12.1 multiply_convert_fusion.12
  841.1 12.8 fusion.24
  862.3 24.3 %copy.73 = bf16[2,1536,1536]{1,0,2:T(2,128)(2,1)} copy(bf16[2,1536,1536]{2,1,0:T(8,128)(2,1)} %pad_maximum_fusion.2) | data formatting | bytes 18874368 | tf_op jit(solution)/shard_map/stack | solution.py:291
  932.3 157.0 %all-reduce.17.cloned.1.call-done = (bf16[1,1024,1536]{2,1,0:T(8,128)(2,1)}, bf16[1,154,1536]{2,1,0:T(8,128)(2,1)}, bf16[1,1024,1536]{2,1,0:T(8,128)(2,1)}, bf16[1,154,1536]{2,1,0:T(8,128)(2,1)}) async-done(((bf16[1,1024,1536]{2,1,0:T(8,128)(2,1)}, bf16[1,154,1536]{2,1,0:T(8,128)(2,1)}, bf16[1,1024,1536]{2,1,0:T(8,128)(2,1)}, bf16[1,154,1536]{2,1,0:T(8,128)(2,1)}), (bf16[1,1024,1536]{2,1,0:T(8,128)(2,1)}, ...) | async-done | bytes 7237648 | tf_op jit(solution)/shard_map/psum | solution.py:239
  1096.4 11.1 fusion.11
  1118.4 9.8 pad_maximum_fusion
  1128.2 35.3 %copy.80 = bf16[2,384,9216]{1,0,2:T(2,128)(2,1)} copy(bf16[2,384,9216]{2,1,0:T(8,128)(2,1)} %pad_maximum_fusion) | data formatting | bytes 28311552
  1163.5 15.5 %copy.93 = bf16[1152,8,2,384]{3,1,2,0:T(8,128)(2,1)} copy(bf16[1152,8,2,384]{3,2,1,0:T(2,128)(2,1)} %bitcast.373) | data formatting | bytes 28311552
  1181.2 74.5 %all-reduce.15.cloned.1.call-done = (bf16[2,384,1536]{1,0,2:T(2,128)(2,1)}, bf16[2,1536,1536]{1,0,2:T(2,128)(2,1)}) async-done(((bf16[2,384,1536]{1,0,2:T(2,128)(2,1)}, bf16[2,1536,1536]{1,0,2:T(2,128)(2,1)}), (bf16[2,384,1536]{1,0,2:T(2,128)(2,1)}, bf16[2,1536,1536]{1,0,2:T(2,128)(2,1)})) %all-reduce.15.cloned.1.call-update) | async-done | bytes 11796496
  1263.8 23.7 %all-reduce.2 = (bf16[2,9216]{1,0:T(2,128)(2,1)S(1)}, bf16[2,2,384]{2,1,0:T(2,128)(2,1)S(1)}, bf16[2,1536]{1,0:T(2,128)(2,1)S(1)}, bf16[2,1536]{1,0:T(2,128)(2,1)S(1)}, bf16[2,1536]{1,0:T(2,128)(2,1)S(1)}) all-reduce(bf16[2,9216]{1,0:T(2,128)(2,1)S(1)} %pad_maximum_fusion.7, ...), channel_id=1, replica_groups=mesh['dp'=8,'tensor'=4] {'dp'}, use_global_device_ids=true, to_apply=%region_45.46 | all-reduce | flops 29184 | bytes 116736 | tf_op jit(solution)/shard_map/psum | solution.py:422
  1301.5 34.6 %reduce-scatter.8.cloned.1.call-done = bf16[2,192,1536]{2,1,0:T(8,128)(2,1)} async-done(((bf16[2,1536,1536]{2,1,0:T(8,128)(2,1)}), bf16[2,192,1536]{2,1,0:T(8,128)(2,1)}) %reduce-scatter.8.cloned.1.call-update) | async-done | bytes 1179664 | tf_op jit(solution)/shard_map/reduce_scatter | solution.py:293
  1339.0 65.8 %reduce-scatter.6.cloned.1.call-done = bf16[2,192,3,384]{3,1,2,0:T(8,128)(2,1)} async-done(((bf16[2,1536,3,384]{3,1,2,0:T(8,128)(2,1)}), bf16[2,192,3,384]{3,1,2,0:T(8,128)(2,1)}) %reduce-scatter.6.cloned.1.call-update) | async-done | bytes 884752 | tf_op jit(solution)/shard_map/reduce_scatter | solution.py:414
  1407.3 102.9 %reduce-scatter.10.cloned.1.call-done = bf16[1152,768]{1,0:T(8,128)(2,1)} async-done(((bf16[9216,768]{1,0:T(8,128)(2,1)}), bf16[1152,768]{1,0:T(8,128)(2,1)}) %reduce-scatter.10.cloned.1.call-update) | async-done | bytes 1769488
  (492 shorter events, 299.3 us)
Async XLA Ops:
  7.2 84.0 %all-gather.6.cloned.1.call-start = ((), (), s32[]{:S(2)}) async-start(), calls=%async_computation.3 | async-start | bytes 15925248 | tf_op jit(solution)/shard_map/all_gather | solution.py:145
  7.9 125.5 %all-reduce.13.cloned.1.call-start = ((), (), s32[]{:S(2)}) async-start(), calls=%async_computation.4 | async-start | bytes 147456 | tf_op jit(solution)/shard_map/psum | solution.py:150
  10.0 81.2 %copy-start.83 = (f32[1,384]{1,0:T(1,128)}, f32[1,384]{1,0:T(1,128)S(1)}, u32[]{:S(2)}) copy-start(f32[1,384]{1,0:T(1,128)S(1)} %get-tuple-element.356) | copy-start | bytes 4612
  99.0 85.0 %all-gather.8.cloned.1.call-start = ((), (), s32[]{:S(2)}) async-start(), calls=%async_computation.5 | async-start | bytes 7962624 | tf_op jit(solution)/shard_map/all_gather | solution.py:146
  99.7 163.3 %all-gather.10.cloned.1.call-start = ((), (), s32[]{:S(2)}) async-start(), calls=%async_computation.6 | async-start | bytes 2654208 | tf_op jit(solution)/shard_map/all_gather | solution.py:147
  100.3 307.4 %all-reduce.21.cloned.1.call-start = ((), (), s32[]{:S(2)}) async-start(), calls=%async_computation.15 | async-start | bytes 7274496 | tf_op jit(solution)/shard_map/psum | solution.py:202
  101.6 85.5 %copy-start.70 = (f32[154]{0:T(256)}, f32[154]{0:T(256)S(1)}, u32[]{:S(2)}) copy-start(f32[154]{0:T(256)S(1)} %broadcast_multiply_fusion.3) | copy-start | bytes 1852
  104.0 89.7 %copy-start.62 = (f32[1024]{0:T(1024)}, f32[1024]{0:T(1024)S(1)}, u32[]{:S(2)}) copy-start(f32[1024]{0:T(1024)S(1)} %broadcast_multiply_fusion.1) | copy-start | bytes 12292
  105.0 88.8 %copy-start.65 = (f32[1024]{0:T(1024)}, f32[1024]{0:T(1024)S(1)}, u32[]{:S(2)}) copy-start(f32[1024]{0:T(1024)S(1)} %fusion.35) | copy-start | bytes 12292
  105.0 88.7 %copy-start.72 = (f32[1024]{0:T(1024)}, f32[1024]{0:T(1024)S(1)}, u32[]{:S(2)}) copy-start(f32[1024]{0:T(1024)S(1)} %fusion.133) | copy-start | bytes 12292
  268.2 139.5 %copy-start.45 = (f32[1536]{0:T(1024)S(1)}, f32[1536]{0:T(1024)}, u32[]{:S(2)}) copy-start(f32[1536]{0:T(1024)} %get-tuple-element.290) | copy-start | bytes 18436
  268.2 142.7 %copy-start.2 = (bf16[1,1024,1536]{2,1,0:T(8,128)(2,1)S(1)}, bf16[1,1024,1536]{2,1,0:T(8,128)(2,1)}, u32[]{:S(2)}) copy-start(bf16[1,1024,1536]{2,1,0:T(8,128)(2,1)} %param.20) | copy-start | bytes 9437188
  268.2 142.7 %copy-start.52 = (f32[1536]{0:T(1024)S(1)}, f32[1536]{0:T(1024)}, u32[]{:S(2)}) copy-start(f32[1536]{0:T(1024)} %get-tuple-element.298) | copy-start | bytes 18436
  270.6 196.6 %all-gather.12.cloned.1.call-start = ((), (), s32[]{:S(2)}) async-start(), calls=%async_computation.7 | async-start | bytes 10616832 | tf_op jit(solution)/shard_map/all_gather | solution.py:197
  271.2 256.6 %all-gather.14.cloned.1.call-start = ((), (), s32[]{:S(2)}) async-start(), calls=%async_computation.8 | async-start | bytes 10616832 | tf_op jit(solution)/shard_map/all_gather | solution.py:198
  272.0 418.8 %all-reduce.19.cloned.1.call-start = ((), (), s32[]{:S(2)}) async-start(), calls=%async_computation.14 | async-start | bytes 7274496 | tf_op jit(solution)/shard_map/psum | solution.py:302
  272.1 433.0 %copy-start.50 = (f32[1536]{0:T(1024)}, f32[1536]{0:T(1024)S(1)}, u32[]{:S(2)}) copy-start(f32[1536]{0:T(1024)S(1)} %get-tuple-element.302) | copy-start | bytes 18436
  272.1 439.2 %copy-start.48 = (f32[1536]{0:T(1024)}, f32[1536]{0:T(1024)S(1)}, u32[]{:S(2)}) copy-start(f32[1536]{0:T(1024)S(1)} %get-tuple-element.301) | copy-start | bytes 18436
  272.2 286.7 %copy-start.99 = (f32[1536]{0:T(1024)}, f32[1536]{0:T(1024)S(1)}, u32[]{:S(2)}) copy-start(f32[1536]{0:T(1024)S(1)} %get-tuple-element.304) | copy-start | bytes 18436
  409.4 283.9 %copy-start.85 = (f32[154]{0:T(256)}, f32[154]{0:T(256)S(1)}, u32[]{:S(2)}) copy-start(f32[154]{0:T(256)S(1)} %broadcast_multiply_fusion.2) | copy-start | bytes 1852
  410.9 282.4 %copy-start.96 = (f32[154]{0:T(256)}, f32[154]{0:T(256)S(1)}, u32[]{:S(2)}) copy-start(f32[154]{0:T(256)S(1)} %fusion.146) | copy-start | bytes 1852
  414.2 290.9 %copy-start.60 = (f32[1024]{0:T(1024)}, f32[1024]{0:T(1024)S(1)}, u32[]{:S(2)}) copy-start(f32[1024]{0:T(1024)S(1)} %broadcast_multiply_fusion) | copy-start | bytes 12292
  415.9 289.1 %copy-start.68 = (f32[1024]{0:T(1024)}, f32[1024]{0:T(1024)S(1)}, u32[]{:S(2)}) copy-start(f32[1024]{0:T(1024)S(1)} %fusion.134) | copy-start | bytes 12292
  553.6 535.6 %all-reduce.17.cloned.1.call-start = ((), (), s32[]{:S(2)}) async-start(), calls=%async_computation.13 | async-start | bytes 14548992 | tf_op jit(solution)/shard_map/psum | solution.py:239
  835.4 420.3 %all-reduce.15.cloned.1.call-start = ((), (), s32[]{:S(2)}) async-start(), calls=%async_computation.12 | async-start | bytes 23592960
  896.1 439.9 %reduce-scatter.8.cloned.1.call-start = ((), (), s32[]{:S(2)}) async-start(), calls=%async_computation.10 | async-start | bytes 10616832 | tf_op jit(solution)/shard_map/reduce_scatter | solution.py:293
  918.4 486.3 %reduce-scatter.6.cloned.1.call-start = ((), (), s32[]{:S(2)}) async-start(), calls=%async_computation.9 | async-start | bytes 7962624 | tf_op jit(solution)/shard_map/reduce_scatter | solution.py:414
  931.4 157.9 %copy-start.59 = (f32[1536]{0:T(1024)S(1)}, f32[1536]{0:T(1024)}, u32[]{:S(2)}) copy-start(f32[1536]{0:T(1024)} %copy-done.58) | copy-start | bytes 18436
  931.4 157.9 %copy-start.63 = (f32[1024]{0:T(1024)S(1)}, f32[1024]{0:T(1024)}, u32[]{:S(2)}) copy-start(f32[1024]{0:T(1024)} %copy-done.62) | copy-start | bytes 12292
  931.4 161.3 %copy-start.66 = (f32[1024]{0:T(1024)S(1)}, f32[1024]{0:T(1024)}, u32[]{:S(2)}) copy-start(f32[1024]{0:T(1024)} %copy-done.65) | copy-start | bytes 12292
  931.4 161.3 %copy-start.73 = (f32[1024]{0:T(1024)S(1)}, f32[1024]{0:T(1024)}, u32[]{:S(2)}) copy-start(f32[1024]{0:T(1024)} %copy-done.72) | copy-start | bytes 12292
  931.5 578.7 %reduce-scatter.10.cloned.1.call-start = ((), (), s32[]{:S(2)}) async-start(), calls=%async_computation.11 | async-start | bytes 15925248
  (118 other events, 1224.6 us)
Sparse Core Ops, SparseCore 0:
  9.9 81.2 all-gather.5
  99.1 34.1 all-reduce.12
  135.3 48.7 all-gather.7
  185.8 28.8 all-gather.9
  270.7 136.9 all-reduce.20
  409.5 57.6 all-gather.11
  469.1 58.6 all-gather.13
  553.8 136.9 all-reduce.18
  835.5 253.6 all-reduce.16
  1093.4 162.2 all-reduce.14
  1259.2 76.7 reduce-scatter.7
  1339.4 65.3 reduce-scatter.5
  1408.3 101.7 reduce-scatter.9
where the time goes:
time: 1540 us; the launch traced here: 1530 us
  waiting for transfers between devices  954 us (62%)
  matrix products  229 us (15%)
  other arithmetic  164 us (11%)
  local copies, waits for them, and re-layouts  136 us (9%)
  blocking collectives  23.7 us (2%)
  between operations  17.5 us (1%)
    unnamed x15, waiting for transfers between devices  181 us
    psum x1, waiting for transfers between devices, shards(): lax.psum(mlp_terms[0].astype(jnp.bfloat16), 'tensor').astype(jnp.float32)  157 us
    psum x1, waiting for transfers between devices, shards(): lax.psum(attn_terms[0].astype(jnp.bfloat16), 'tensor').astype(jnp.float32)  136 us
    psum x1, waiting for transfers between devices, shards(): lax.psum(mid_terms[0].astype(jnp.bfloat16), 'tensor').astype(jnp.float32)  121 us
    all_gather x1, waiting for transfers between devices, shards(): lax.all_gather(ada_weight, 'dp', axis=2, tiled=True)  81.2 us
    unnamed x244, local copies, waits for them, and re-layouts  67.6 us
    reduce_scatter x1, waiting for transfers between devices, shards(): lax.psum_scatter(qkv_grad_all.astype(jnp.bfloat16), 'dp', scatter_dimensi...  65.8 us
    all_gather x1, waiting for transfers between devices, shards(): lax.all_gather(mlp_in_weight, 'dp', axis=1, tiled=True)  51.3 us
  transfers between devices with their start and end apart: 13, of which 12 were waited for; matrix products, arithmetic and copies ran while one was open for 22% of the time, Pallas kernels for 0%

commit v1 on v0

--- a/solution.py
+++ b/solution.py
@@ -1,12 +1,115 @@
+import functools
 import math
 
 import jax
 import jax.numpy as jnp
 from jax import lax
+from jax.experimental import pallas as pl
+from jax.experimental.pallas import tpu as pltpu
 from jax.sharding import PartitionSpec as P
 
 D = 1536
 HEAD_DIM = 64
+
+
+MESH = pl.DeviceIdType.MESH
+ROWS = 1184
+
+
+def ar_kernel(n, R, x_ref, o_ref, rin, rx, pb, s1, s2, r1, r2, r3):
+    NC = ROWS // R
+    me = lax.axis_index("tensor")
+    half = n // 2
+    left = me < half
+    is_mid = (me == half - 1) | (me == half)
+    inward = jnp.where(left, me + 1, me - 1)
+    outward = jnp.where(left, me - 1, me + 1)
+    bar = pltpu.get_barrier_semaphore()
+    pl.semaphore_signal(bar, inc=1, device_id={"tensor": inward}, device_id_type=MESH)
+
+    @pl.when(is_mid)
+    def _():
+        pl.semaphore_signal(bar, inc=1, device_id={"tensor": outward}, device_id_type=MESH)
+        pl.semaphore_wait(bar, 2)
+
+    @pl.when(jnp.logical_not(is_mid))
+    def _():
+        pl.semaphore_wait(bar, 1)
+
+    def sl(k):
+        return pl.ds(pl.multiple_of(k * R, R), R)
+
+    def to_mid(k):
+        return pltpu.make_async_remote_copy(x_ref.at[sl(k)], rin.at[sl(k)], s1.at[k], r1.at[k],
+                                            device_id={"tensor": inward}, device_id_type=MESH)
+    def xchg(k):
+        return pltpu.make_async_remote_copy(pb.at[sl(k)], rx.at[sl(k)], s1.at[k], r2.at[k],
+                                            device_id={"tensor": inward}, device_id_type=MESH)
+    def out(k):
+        return pltpu.make_async_remote_copy(o_ref.at[sl(k)], o_ref.at[sl(k)], s2.at[k], r3.at[k],
+                                            device_id={"tensor": outward}, device_id_type=MESH)
+
+    @pl.when(jnp.logical_not(is_mid))
+    def _():
+        def send(k, c):
+            to_mid(k).start()
+            return c
+        lax.fori_loop(0, NC, send, 0)
+        def fin(k, c):
+            out(k).wait_recv()
+            to_mid(k).wait_send()
+            return c
+        lax.fori_loop(0, NC, fin, 0)
+
+    @pl.when(is_mid)
+    def _():
+        def a(k):
+            to_mid(k).wait_recv()
+            pb[sl(k)] = (x_ref[sl(k)].astype(jnp.float32) + rin[sl(k)].astype(jnp.float32)).astype(jnp.bfloat16)
+            xchg(k).start()
+        def b(k):
+            xchg(k).wait_recv()
+            o_ref[sl(k)] = (pb[sl(k)].astype(jnp.float32) + rx[sl(k)].astype(jnp.float32)).astype(jnp.bfloat16)
+            out(k).start()
+        L = 2
+        for k in range(L):
+            a(k)
+        def st(k, c):
+            a(k)
+            b(k - L)
+            return c
+        lax.fori_loop(L, NC, st, 0)
+        for k in range(NC - L, NC):
+            b(k)
+        def fin(k, c):
+            xchg(k).wait_send()
+            out(k).wait_send()
+            return c
+        lax.fori_loop(0, NC, fin, 0)
+
+def ar(x, n, R, cid):
+    NC = ROWS // R
+    V = lambda: pltpu.VMEM((ROWS, D), jnp.bfloat16)
+    S = lambda: pltpu.SemaphoreType.DMA((NC,))
+    return pl.pallas_call(
+        functools.partial(ar_kernel, n, R),
+        out_shape=jax.ShapeDtypeStruct((ROWS, D), jnp.bfloat16),
+        in_specs=[pl.BlockSpec(memory_space=pltpu.VMEM)],
+        out_specs=pl.BlockSpec(memory_space=pltpu.VMEM),
+        scratch_shapes=[V(), V(), V(), S(), S(), S(), S(), S()],
+        compiler_params=pltpu.CompilerParams(collective_id=cid, has_side_effects=True, vmem_limit_bytes=60 << 20),
+    )(x)
+
+def z_sum(image_part, text_part, size, cid):
+    li, lt = image_part.shape[1], text_part.shape[1]
+    joint = jnp.concatenate(
+        [image_part[0], text_part[0], jnp.zeros((ROWS - li - lt, D), jnp.float32)]
+    ).astype(jnp.bfloat16)
+    total = ar(joint, size, 32, cid)
+    return (
+        total[None, :li].astype(jnp.float32),
+        total[None, li : li + lt].astype(jnp.float32),
+    )
 
 
 def layer_norm(inputs):
@@ -141,12 +244,14 @@
     condition = pooled.astype(jnp.float32) + time_embed(timestep, first_col, width_local)
     cond_act, silu_pull = jax.vjp(jax.nn.silu, condition)
     cond_low = cond_act.astype(jnp.bfloat16)
-    ada_full, query_key_value_whole, out_full = (
-        lax.all_gather(ada_weight, "dp", axis=2, tiled=True),
+    size = lax.axis_size("tensor")
+    cond_all = lax.all_gather(cond_low, "dp", axis=0, tiled=True)
+    query_key_value_whole, out_full = (
         lax.all_gather(qkv_weight, "dp", axis=1, tiled=True),
         lax.all_gather(out_weight, "dp", axis=2, tiled=True),
     )
-    mod_part = jnp.einsum("sc,nce->nse", cond_low, ada_full, preferred_element_type=jnp.float32)
+    mod_part = jnp.einsum("sc,nce->nse", cond_all, ada_weight, preferred_element_type=jnp.float32)
+    mod_part = lax.all_to_all(mod_part, "dp", split_axis=1, concat_axis=2, tiled=True)
     modul = lax.psum(mod_part, "tensor") + ada_bias.astype(jnp.float32)[:, None, :]
     seq_count = modul.shape[1]
     modul = modul.reshape(2, seq_count, 6, 1, D)
@@ -198,10 +303,8 @@
         lax.all_gather(mlp_out_weight, "dp", axis=2, tiled=True),
     )
     branches, resids, second_pulls, lowered_middle_list = ([], [], [], [])
-    attn_sum = (
-        lax.psum(attn_terms[0].astype(jnp.bfloat16), "tensor").astype(jnp.float32),
-        lax.psum(attn_terms[1].astype(jnp.bfloat16), "tensor").astype(jnp.float32),
-    )
+    attn_terms = tuple(attn_terms)
+    attn_sum = z_sum(attn_terms[0], attn_terms[1], size, 1)
     for modality_branch in range(2):
         branch = attn_sum[modality_branch] + out_bias_f[modality_branch]
         resid = streams[modality_branch] + modul[modality_branch, :, 2] * branch
@@ -235,10 +338,7 @@
         )
         gelu_pulls.append(gelu_pull)
         activation_lowered_list.append(activation_lowered)
-    mlp_sum = (
-        lax.psum(mlp_terms[0].astype(jnp.bfloat16), "tensor").astype(jnp.float32),
-        lax.psum(mlp_terms[1].astype(jnp.bfloat16), "tensor").astype(jnp.float32),
-    )
+    mlp_sum = z_sum(mlp_terms[0], mlp_terms[1], size, 2)
     block_out, gate2_grads = ([], [])
     for modality_branch in range(2):
         second_branch = mlp_sum[modality_branch] + last_bias_f[modality_branch]
@@ -256,7 +356,7 @@
         mlp_gradient_lowered = d_mlp.astype(jnp.bfloat16)
         w_out_grads.append(
             jnp.einsum(
-                "equ,eqo->uo",
+                "equ,eqo->ou",
                 activation_lowered_list[modality_branch],
                 mlp_gradient_lowered,
                 preferred_element_type=jnp.float32,
@@ -293,15 +393,16 @@
         lax.psum_scatter(
             w_in_grad_all.astype(jnp.bfloat16), "dp", scatter_dimension=1, tiled=True
         ).astype(jnp.float32),
-        lax.psum_scatter(
-            w_out_grad_all.astype(jnp.bfloat16), "dp", scatter_dimension=2, tiled=True
-        ).astype(jnp.float32),
+        jnp.swapaxes(
+            lax.psum_scatter(
+                w_out_grad_all.astype(jnp.bfloat16), "dp", scatter_dimension=1, tiled=True
+            ).astype(jnp.float32),
+            1,
+            2,
+        ),
     )
     d_resids, shift2_grads, scale2_grads, gate1_grads, outb_grads = ([], [], [], [], [])
-    d_mid = (
-        lax.psum(mid_terms[0].astype(jnp.bfloat16), "tensor").astype(jnp.float32),
-        lax.psum(mid_terms[1].astype(jnp.bfloat16), "tensor").astype(jnp.float32),
-    )
+    d_mid = z_sum(mid_terms[0], mid_terms[1], size, 3)
     d_attn_lows = []
     for modality_branch in range(2):
         d_resid, shift_two, scale_two = second_pulls[modality_branch](d_mid[modality_branch])
@@ -317,7 +418,7 @@
     for modality_branch in range(2):
         out_grads.append(
             jnp.einsum(
-                "kyb,kyt->bt",
+                "kyb,kyt->tb",
                 mix_parts[modality_branch],
                 d_attn_lows[modality_branch],
                 preferred_element_type=jnp.float32,
@@ -371,10 +472,7 @@
                 preferred_element_type=jnp.float32,
             )
         )
-    d_in = (
-        lax.psum(in_terms[0].astype(jnp.bfloat16), "tensor").astype(jnp.float32),
-        lax.psum(in_terms[1].astype(jnp.bfloat16), "tensor").astype(jnp.float32),
-    )
+    d_in = z_sum(in_terms[0], in_terms[1], size, 4)
     token_grads, d_mods = ([], [])
     for modality_branch in range(2):
         d_tokens, shift_one, scale_one = first_pulls[modality_branch](d_in[modality_branch])
@@ -392,38 +490,50 @@
                 axis=1,
             )
         )
-    ada_grads, adab_grads = ([], [])
-    d_cond_act = jnp.zeros(cond_act.shape, jnp.float32)
-    for modality_branch in range(2):
-        d_mod_low = d_mods[modality_branch].reshape(seq_count, 6 * D).astype(jnp.bfloat16)
-        adab_grads.append(jnp.sum(d_mod_low.astype(jnp.float32), axis=0))
-        ada_grads.append(
-            jnp.einsum("sc,se->ce", cond_low, d_mod_low, preferred_element_type=jnp.float32)
-        )
-        d_cond_act = d_cond_act + jnp.einsum(
-            "se,ce->sc", d_mod_low, ada_full[modality_branch], preferred_element_type=jnp.float32
-        )
+    small = [
+        jnp.concatenate([d_mods[0].reshape(-1), d_mods[1].reshape(-1)]),
+        jnp.stack(pair_grads).reshape(-1),
+        jnp.stack(outb_grads).reshape(-1),
+        jnp.stack(bias1_grads).reshape(-1),
+        jnp.stack(bias2_grads).reshape(-1),
+    ]
+    every = lax.all_gather(jnp.concatenate(small).astype(jnp.bfloat16), "dp")
+    summed = jnp.sum(every.astype(jnp.float32), axis=0)
+    at = [0]
+    for part in small:
+        at.append(at[-1] + part.shape[0])
+    adab_sum = summed[: at[1]].reshape(2, 6 * D)
+    pair_sum = summed[at[1] : at[2]].reshape(2, 2, -1)
+    outb_sum = summed[at[2] : at[3]].reshape(2, -1)
+    bias1_sum = summed[at[3] : at[4]].reshape(2, -1)
+    bias2_sum = summed[at[4] :].reshape(2, -1)
+    cols = ada_weight.shape[2]
+    d_mod_cols = lax.dynamic_slice_in_dim(
+        every[:, : at[1]].reshape(-1, 2, 6 * D), lax.axis_index("dp") * cols, cols, axis=2
+    )
+    ada_shard = jnp.einsum(
+        "sc,sne->nce", cond_all, d_mod_cols, preferred_element_type=jnp.float32
+    )
+    d_cond_act = lax.psum_scatter(
+        jnp.einsum("sne,nce->sc", d_mod_cols, ada_weight, preferred_element_type=jnp.float32),
+        "dp",
+        scatter_dimension=0,
+        tiled=True,
+    )
     (pooled_grad,) = silu_pull(d_cond_act)
-    ada_grad_all = jnp.stack(ada_grads)
     qkv_grad_all = jnp.stack(qkv_grads)
     out_grad_all = jnp.stack(out_grads)
-    ada_shard, qkv_shard, out_shard = (
-        lax.psum_scatter(
-            ada_grad_all.astype(jnp.bfloat16), "dp", scatter_dimension=2, tiled=True
-        ).astype(jnp.float32),
+    qkv_shard, out_shard = (
         lax.psum_scatter(
             qkv_grad_all.astype(jnp.bfloat16), "dp", scatter_dimension=1, tiled=True
         ).astype(jnp.float32),
-        lax.psum_scatter(
-            out_grad_all.astype(jnp.bfloat16), "dp", scatter_dimension=2, tiled=True
-        ).astype(jnp.float32),
-    )
-    adab_sum, pair_sum, outb_sum, bias1_sum, bias2_sum = (
-        lax.psum(jnp.stack(adab_grads).astype(jnp.bfloat16), "dp").astype(jnp.float32),
-        lax.psum(jnp.stack(pair_grads).astype(jnp.bfloat16), "dp").astype(jnp.float32),
-        lax.psum(jnp.stack(outb_grads).astype(jnp.bfloat16), "dp").astype(jnp.float32),
-        lax.psum(jnp.stack(bias1_grads).astype(jnp.bfloat16), "dp").astype(jnp.float32),
-        lax.psum(jnp.stack(bias2_grads).astype(jnp.bfloat16), "dp").astype(jnp.float32),
+        jnp.swapaxes(
+            lax.psum_scatter(
+                out_grad_all.astype(jnp.bfloat16), "dp", scatter_dimension=1, tiled=True
+            ).astype(jnp.float32),
+            1,
+            2,
+        ),
     )
     return (
         block_out[0],

time: 1540 us -> 1040 us (0.68)
  waiting for transfers between devices: 954 us -> 41.3 us
  Pallas kernels: 0 us -> 373 us
  blocking collectives: 23.7 us -> 56.8 us
  matrix products: 229 us -> 209 us
  local copies, waits for them, and re-layouts: 136 us -> 154 us
    psum x3 -> x0, waiting for transfers between devices: 414 us -> none  [the longest x1 157 us: shards(): lax.psum(mlp_terms[0].astype(jnp.bfloat16), 'tensor').astype(jnp.float32)]
    pallas_call x0 -> x4, Pallas kernels: none -> 373 us  [ar(): pl.pallas_call(functools.partial(ar_kernel, n, R), out_shape=jax.ShapeDty...]
    unnamed x15 -> x9, waiting for transfers between devices: 181 us -> 2.34 us
    all_gather x1 -> x0, waiting for transfers between devices: 81.2 us -> none  [shards(): lax.all_gather(ada_weight, 'dp', axis=2, tiled=True)]
    concatenate x0 -> x6, local copies, waits for them, and re-layouts: none -> 73.9 us  [the longest x4 73.3 us: z_sum(): jnp.concatenate([image_part[0], text_part[0], jnp.zeros((ROWS - li - lt,...]
    reduce_scatter x1, waiting for transfers between devices: 65.8 us -> 0.01 us  [shards(): lax.psum_scatter(qkv_grad_all.astype(jnp.bfloat16), 'dp', scatter_dimensi...]
    all_gather x1, waiting for transfers between devices: 51.3 us -> 0.03 us  [shards(): lax.all_gather(mlp_in_weight, 'dp', axis=1, tiled=True)]
    all_gather x1, waiting for transfers between devices: 49.8 us -> 0.01 us  [shards(): lax.all_gather(mlp_out_weight, 'dp', axis=2, tiled=True)]
  transfers between devices with their start and end apart: 13 -> 9, of which waited for: 12 -> 2; matrix products, arithmetic and copies ran while one was open for 22% -> 37% of each run, Pallas kernels for 0% -> 18%
where the time goes in v1:
time: 1040 us; the launch traced here: 1030 us
  Pallas kernels  373 us (36%)
  matrix products  209 us (20%)
  other arithmetic  172 us (17%)
  local copies, waits for them, and re-layouts  154 us (15%)
  blocking collectives  56.8 us (5%)
  waiting for transfers between devices  41.3 us (4%)
  between operations  18.8 us (2%)
    pallas_call x4, Pallas kernels, ar(): pl.pallas_call(functools.partial(ar_kernel, n, R), out_shape=jax.ShapeDty...  373 us
    concatenate x4, local copies, waits for them, and re-layouts, z_sum(): jnp.concatenate([image_part[0], text_part[0], jnp.zeros((ROWS - li - lt,...  73.3 us
    dot_general x2, matrix products, attend_block_back(): jnp.einsum('qhd,khd->hqk', g_heads, v_heads, preferred_element_type=jnp.f...  24.5 us
    convert_element_type x2, other arithmetic, attend_block_back(): grad_score = (prob_rows * (grad_prob - row_delta)).astype(jnp.bfloat16)  24.4 us
    reduce_sum x8, other arithmetic, modulate(): return layer_norm(inputs) * (1.0 + scale_by) + shift_by  24.3 us
    psum x1, waiting for transfers between devices, shards(): lax.psum(mod_part, 'tensor') + ada_bias.astype(jnp.float32)[:, None, :]  24.1 us
    unnamed x1, blocking collectives  23.5 us
  transfers between devices with their start and end apart: 9, of which 2 were waited for; matrix products, arithmetic and copies ran while one was open for 37% of the time, Pallas kernels for 18%

profile of v1, /device:TPU:0, one launch (start us, length us, event | category | flops | bytes accessed | tf_op | source)
XLA Modules:
  0.0 1026.5 jit_solution(13443928277842501706)
XLA Ops:
  10.2 10.4 %all-gather = bf16[8,1,384]{2,1,0:T(2,128)(2,1)S(1)} all-gather(bf16[1,1,384]{2,1,0:T(2,128)(2,1)S(1)} %get-tuple-element.371), channel_id=1, replica_groups=mesh['dp'=8,'tensor'=4] {'dp'}, dimensions={0}, use_global_device_ids=true | all-gather | bytes 6912 | tf_op jit(solution)/shard_map/all_gather | solution.py:248
  38.8 24.1 %all-reduce.3.cloned.1.call-done = f32[2,1,9216]{2,0,1:T(2,128)} async-done(((f32[2,1,9216]{2,0,1:T(2,128)}), f32[2,1,9216]{2,0,1:T(2,128)}) %all-reduce.3.cloned.1.call-update) | async-done | bytes 73744 | tf_op jit(solution)/shard_map/psum | solution.py:255
  64.7 14.8 %all-gather.7.cloned.1.call-done = bf16[2,1536,3,384]{3,1,2,0:T(8,128)(2,1)} async-done(((bf16[2,192,3,384]{3,1,2,0:T(8,128)(2,1)}), bf16[2,1536,3,384]{3,1,2,0:T(8,128)(2,1)}) %all-gather.7.cloned.1.call-update) | async-done | bytes 7077904 | tf_op jit(solution)/shard_map/all_gather | solution.py:250
  106.9 61.2 %while.47 = (s32[]{:T(128)}, bf16[2,589,384]{2,1,0:T(8,128)(2,1)}, f32[2,6,589]{2,1,0:T(8,128)}, bf16[2,589,384]{1,2,0:T(8,128)(2,1)}, bf16[1178,384]{0,1:T(8,12...) while((s32[]{:T(128)}, bf16[2,589,384]{2,1,0:T(8,128)(2,1)}, f32[2,6,589]{2,1,0:T(8,128)}, ...), condition=%wide.region_8.9_spmd, body=%wide.region_5.8_spmd.sunk | while | flops 1095105280 | bytes 55745600 | solution.py:163
  108.0 8.8 fusion.214
  116.8 10.0 fusion.215
  126.9 8.9 fusion.216
  138.9 9.1 fusion.214
  148.0 9.0 fusion.215
  157.0 8.9 fusion.216
  178.0 18.3 %concatenate.54.x_ref = bf16[1184,1536]{1,0:T(8,128)(2,1)} concatenate(bf16[1024,1536]{1,0:T(8,128)(2,1)} %convolution_convert_fusion.6, bf16[154,1536]{1,0:T(8,128)(2,1)} %convolution_convert_fusion.9, bf16[6,1536]{1,0:T(8,128)(2,1)S(1)} %broadcast.494), dimensions={0} | concatenate | bytes 7274496 | tf_op jit(solution)/shard_map/concatenate | solution.py:105
  196.3 96.3 %shard_map.271 = bf16[1184,1536]{1,0:T(8,128)(2,1)} custom-call(bf16[1184,1536]{1,0:T(8,128)(2,1)} %concatenate.54.x_ref), custom_call_target="tpu_custom_call" | custom-call | tf_op jit(solution)/shard_map/pallas_call | solution.py:94
  324.0 9.3 fusion.174
  334.9 9.0 fusion.53
  343.9 18.2 %concatenate.56.x_ref = bf16[1184,1536]{1,0:T(8,128)(2,1)} concatenate(bf16[1024,1536]{1,0:T(8,128)(2,1)} %fusion.53, bf16[154,1536]{1,0:T(8,128)(2,1)} %fusion.71, bf16[6,1536]{1,0:T(8,128)(2,1)S(1)} %broadcast.494), dimensions={0} | concatenate | bytes 7274496 | tf_op jit(solution)/shard_map/concatenate | solution.py:105
  362.1 92.9 %shard_map.273 = bf16[1184,1536]{1,0:T(8,128)(2,1)} custom-call(bf16[1184,1536]{1,0:T(8,128)(2,1)} %concatenate.56.x_ref), custom_call_target="tpu_custom_call" | custom-call | tf_op jit(solution)/shard_map/pallas_call | solution.py:94
  468.6 9.0 fusion.52
  477.6 18.3 %concatenate.55.x_ref = bf16[1184,1536]{1,0:T(8,128)(2,1)} concatenate(bf16[1024,1536]{1,0:T(8,128)(2,1)} %fusion.52, bf16[154,1536]{1,0:T(8,128)(2,1)} %fusion.70, bf16[6,1536]{1,0:T(8,128)(2,1)S(1)} %broadcast.494), dimensions={0} | concatenate | bytes 7274496 | tf_op jit(solution)/shard_map/concatenate | solution.py:105
  495.9 91.9 %shard_map.272 = bf16[1184,1536]{1,0:T(8,128)(2,1)} custom-call(bf16[1184,1536]{1,0:T(8,128)(2,1)} %concatenate.55.x_ref), custom_call_target="tpu_custom_call" | custom-call | tf_op jit(solution)/shard_map/pallas_call | solution.py:94
  597.2 10.0 fusion.169
  622.6 96.8 %while.48 = (s32[]{:T(128)}, f32[1178,384]{0,1:T(8,128)}, f32[1178,384]{0,1:T(8,128)}, bf16[2,589,384]{1,2,0:T(8,128)(2,1)}, bf16[2,589,384]{1,2,0:T(8,128)(2,1)...) while((s32[]{:T(128)}, f32[1178,384]{0,1:T(8,128)}, ...), condition=%wide.region_19.20_spmd.clone, body=%wide.region_17.19_spmd.clone.sunk | while | flops 2700368384 | bytes 256336176 | solution.py:214
  638.3 12.9 %multiply_reduce_fusion.6 = (f32[6,589]{1,0:T(8,128)S(1)}, f32[6,589,1178]{2,1,0:T(8,128)}) fusion(f32[6,589,1178]{2,1,0:T(8,128)} %copy-done.1, bf16[589,6,64]{0,2,1:T(8,128)(2,1)S(1)} %bitcast.479, bf16[1178,6,64]{0,2,1:T(8,128)(2,1)S(1)} %bitcast.482), kind=kOutput, calls=%fused_computation.12.clone.1 | convolution fusion | flops 541193216 | bytes 34675608 | tf_op jit(solution)/shard_map/while/body/eval_jaxpr/while/body/eval_jaxpr/qhd,khd->hqk/dot_general | solution.py:179
  651.3 12.3 %multiply_convert_fusion.10 = bf16[6,589,1178]{2,1,0:T(8,128)(2,1)S(1)} fusion(f32[6,589,1178]{2,1,0:T(8,128)} %copy-done.1, f32[6,589,1178]{2,1,0:T(8,128)} %get-tuple-element.507, f32[6,589]{1,0:T(8,128)S(1)} %get-tuple-element.508), kind=kLoop, calls=%fused_computation.11.clone.1 | loop fusion | flops 12489156 | bytes 41644656 | tf_op jit(solution)/shard_map/while/body/eval_jaxpr/while/body/eval_jaxpr/convert_element_type | solution.py:181
  687.1 11.5 %multiply_reduce_fusion.6 = (f32[6,589]{1,0:T(8,128)S(1)}, f32[6,589,1178]{2,1,0:T(8,128)}) fusion(f32[6,589,1178]{2,1,0:T(8,128)} %copy-done.1, bf16[589,6,64]{0,2,1:T(8,128)(2,1)S(1)} %bitcast.479, bf16[1178,6,64]{0,2,1:T(8,128)(2,1)S(1)} %bitcast.482), kind=kOutput, calls=%fused_computation.12.clone.1 | convolution fusion | flops 541193216 | bytes 34675608 | tf_op jit(solution)/shard_map/while/body/eval_jaxpr/while/body/eval_jaxpr/qhd,khd->hqk/dot_general | solution.py:179
  698.6 12.1 %multiply_convert_fusion.10 = bf16[6,589,1178]{2,1,0:T(8,128)(2,1)S(1)} fusion(f32[6,589,1178]{2,1,0:T(8,128)} %copy-done.1, f32[6,589,1178]{2,1,0:T(8,128)} %get-tuple-element.507, f32[6,589]{1,0:T(8,128)S(1)} %get-tuple-element.508), kind=kLoop, calls=%fused_computation.11.clone.1 | loop fusion | flops 12489156 | bytes 41644656 | tf_op jit(solution)/shard_map/while/body/eval_jaxpr/while/body/eval_jaxpr/convert_element_type | solution.py:181
  750.8 11.7 %fusion.22 = bf16[1,1536,1536]{2,1,0:T(8,128)(2,1)} fusion(bf16[1,1024,1536]{2,1,0:T(8,128)(2,1)S(1)} %copy-done.29, f32[1536]{0:T(1024)S(1)} %copy-done.68, f32[1024,1536]{1,0:T(8,128)} %copy-done.144, f32[1536]{0:T(1024)S(1)} %copy-done.119), kind=kOutput, calls=%fused_computation.60 | convolution fusion | flops 4854644736 | bytes 14168064 | tf_op jit(solution)/shard_map/equ,eqo->ou/dot_general | solution.py:358
  785.0 8.3 pad_maximum_fusion
  810.2 8.4 bitcast_convert_fusion
  818.6 18.5 %concatenate.58.x_ref = bf16[1184,1536]{1,0:T(8,128)(2,1)} concatenate(bf16[1024,1536]{1,0:T(8,128)(2,1)} %bitcast_convert_fusion, bf16[154,1536]{1,0:T(8,128)(2,1)} %fusion.72, bf16[6,1536]{1,0:T(8,128)(2,1)S(1)} %copy-done.41), dimensions={0} | concatenate | bytes 7274496 | tf_op jit(solution)/shard_map/concatenate | solution.py:105
  837.1 92.1 %shard_map.274 = bf16[1184,1536]{1,0:T(8,128)(2,1)} custom-call(bf16[1184,1536]{1,0:T(8,128)(2,1)} %concatenate.58.x_ref), custom_call_target="tpu_custom_call" | custom-call | tf_op jit(solution)/shard_map/pallas_call | solution.py:94
  945.4 14.8 %all-gather.1 = bf16[8,1,29184]{2,1,0:T(2,128)(2,1)S(1)} all-gather(bf16[1,1,29184]{2,1,0:T(2,128)(2,1)S(1)} %bitcast.492), channel_id=1, replica_groups=mesh['dp'=8,'tensor'=4] {'dp'}, dimensions={0}, use_global_device_ids=true | all-gather | bytes 525312 | tf_op jit(solution)/shard_map/all_gather | solution.py:500
  976.0 23.5 %all-reduce = f32[8,384]{1,0:T(8,128)S(1)} all-reduce(f32[8,384]{1,0:T(8,128)S(1)} %convolution_bitcast_fusion.2), channel_id=2, replica_groups=mesh['dp'=8,'tensor'=4] {'dp'}, use_global_device_ids=true, to_apply=%region_46.47.clone | all-reduce | flops 3072 | bytes 24576
  (550 shorter events, 303.7 us)
Async XLA Ops:
  8.0 54.9 %all-reduce.3.cloned.1.call-start = ((), (), s32[]{:S(2)}) async-start(), calls=%async_computation.5 | async-start | bytes 147456 | tf_op jit(solution)/shard_map/psum | solution.py:255
  20.7 42.3 %copy-start.83 = (bf16[2,9216]{1,0:T(2,128)(2,1)S(1)}, bf16[2,9216]{1,0:T(2,128)(2,1)}, u32[]{:S(2)}) copy-start(bf16[2,9216]{1,0:T(2,128)(2,1)} %param.27) | copy-start | bytes 110596
  29.2 50.4 %all-gather.7.cloned.1.call-start = ((), (), s32[]{:S(2)}) async-start(), calls=%async_computation.6 | async-start | bytes 7962624 | tf_op jit(solution)/shard_map/all_gather | solution.py:250
  29.8 140.5 %all-gather.9.cloned.1.call-start = ((), (), s32[]{:S(2)}) async-start(), calls=%async_computation.7 | async-start | bytes 2654208 | tf_op jit(solution)/shard_map/all_gather | solution.py:251
  30.4 272.8 %all-gather.11.cloned.1.call-start = ((), (), s32[]{:S(2)}) async-start(), calls=%async_computation.8 | async-start | bytes 10616832 | tf_op jit(solution)/shard_map/all_gather | solution.py:302
  31.0 276.7 %all-gather.13.cloned.1.call-start = ((), (), s32[]{:S(2)}) async-start(), calls=%async_computation.9 | async-start | bytes 10616832 | tf_op jit(solution)/shard_map/all_gather | solution.py:303
  31.7 976.6 %reduce-scatter.7.cloned.1.call-start = ((), (), s32[]{:S(2)}) async-start(), calls=%async_computation.11 | async-start | bytes 2654208 | tf_op jit(solution)/shard_map/reduce_scatter | solution.py:531
  33.2 49.5 %copy-start.84 = (f32[154]{0:T(256)}, f32[154]{0:T(256)S(1)}, u32[]{:S(2)}) copy-start(f32[154]{0:T(256)S(1)} %broadcast_multiply_fusion.3) | copy-start | bytes 1852
  33.5 49.2 %copy-start.91 = (f32[154]{0:T(256)}, f32[154]{0:T(256)S(1)}, u32[]{:S(2)}) copy-start(f32[154]{0:T(256)S(1)} %fusion.150) | copy-start | bytes 1852
  35.9 53.4 %copy-start.60 = (f32[1024]{0:T(1024)}, f32[1024]{0:T(1024)S(1)}, u32[]{:S(2)}) copy-start(f32[1024]{0:T(1024)S(1)} %broadcast_multiply_fusion.1) | copy-start | bytes 12292
  36.9 52.4 %copy-start.69 = (f32[1024]{0:T(1024)}, f32[1024]{0:T(1024)S(1)}, u32[]{:S(2)}) copy-start(f32[1024]{0:T(1024)S(1)} %fusion.139) | copy-start | bytes 12292
  178.0 299.6 %copy-start.40 = (bf16[6,1536]{1,0:T(8,128)(2,1)}, bf16[6,1536]{1,0:T(8,128)(2,1)S(1)}, u32[]{:S(2)}) copy-start(bf16[6,1536]{1,0:T(8,128)(2,1)S(1)} %broadcast.494) | copy-start | bytes 55300
  178.0 114.7 %copy-start.21 = (bf16[1,154,1536]{2,1,0:T(8,128)(2,1)S(1)}, bf16[1,154,1536]{2,1,0:T(8,128)(2,1)}, u32[]{:S(2)}) copy-start(bf16[1,154,1536]{2,1,0:T(8,128)(2,1)} %param.21) | copy-start | bytes 1419268
  178.0 114.7 %copy-start.38 = (f32[1536]{0:T(1024)S(1)}, f32[1536]{0:T(1024)}, u32[]{:S(2)}) copy-start(f32[1536]{0:T(1024)} %get-tuple-element.316) | copy-start | bytes 18436
  178.0 114.7 %copy-start.45 = (f32[1536]{0:T(1024)S(1)}, f32[1536]{0:T(1024)}, u32[]{:S(2)}) copy-start(f32[1536]{0:T(1024)} %get-tuple-element.406) | copy-start | bytes 18436
  196.3 99.9 %copy-start.47 = (f32[1536]{0:T(1024)S(1)}, f32[1536]{0:T(1024)}, u32[]{:S(2)}) copy-start(f32[1536]{0:T(1024)} %get-tuple-element.405) | copy-start | bytes 18436
  196.3 99.9 %copy-start.49 = (f32[1536]{0:T(1024)S(1)}, f32[1536]{0:T(1024)}, u32[]{:S(2)}) copy-start(f32[1536]{0:T(1024)} %get-tuple-element.324) | copy-start | bytes 18436
  294.2 296.3 %copy-start.89 = (f32[154]{0:T(256)}, f32[154]{0:T(256)S(1)}, u32[]{:S(2)}) copy-start(f32[154]{0:T(256)S(1)} %broadcast_multiply_fusion.2) | copy-start | bytes 1852
  296.2 294.3 %copy-start.102 = (f32[154]{0:T(256)}, f32[154]{0:T(256)S(1)}, u32[]{:S(2)}) copy-start(f32[154]{0:T(256)S(1)} %fusion.151) | copy-start | bytes 1852
  300.4 296.8 %copy-start.72 = (f32[1024]{0:T(1024)}, f32[1024]{0:T(1024)S(1)}, u32[]{:S(2)}) copy-start(f32[1024]{0:T(1024)S(1)} %broadcast_multiply_fusion) | copy-start | bytes 12292
  303.1 294.0 %copy-start.79 = (f32[1024]{0:T(1024)}, f32[1024]{0:T(1024)S(1)}, u32[]{:S(2)}) copy-start(f32[1024]{0:T(1024)S(1)} %fusion.140) | copy-start | bytes 12292
  477.6 112.9 %copy-start.87 = (f32[1536]{0:T(1024)S(1)}, f32[1536]{0:T(1024)}, u32[]{:S(2)}) copy-start(f32[1536]{0:T(1024)} %get-tuple-element.325) | copy-start | bytes 18436
  495.9 94.6 %copy-start.43 = (bf16[1,154,1536]{2,1,0:T(8,128)(2,1)S(1)}, bf16[1,154,1536]{2,1,0:T(8,128)(2,1)}, u32[]{:S(2)}) copy-start(bf16[1,154,1536]{2,1,0:T(8,128)(2,1)} %param.25) | copy-start | bytes 1419268
  495.9 101.3 %copy-start.86 = (f32[1536]{0:T(1024)S(1)}, f32[1536]{0:T(1024)}, u32[]{:S(2)}) copy-start(f32[1536]{0:T(1024)} %get-tuple-element.326) | copy-start | bytes 18436
  622.6 387.6 %reduce-scatter.5.cloned.1.call-start = ((), (), s32[]{:S(2)}) async-start(), calls=%async_computation.10 | async-start | bytes 7962624 | tf_op jit(solution)/shard_map/reduce_scatter | solution.py:527
  744.7 268.0 %reduce-scatter.11.cloned.1.call-start = ((), (), s32[]{:S(2)}) async-start(), calls=%async_computation.13 | async-start | bytes 10616832 | tf_op jit(solution)/shard_map/reduce_scatter | solution.py:397
  770.9 244.7 %reduce-scatter.9.cloned.1.call-start = ((), (), s32[]{:S(2)}) async-start(), calls=%async_computation.12 | async-start | bytes 10616832 | tf_op jit(solution)/shard_map/reduce_scatter | solution.py:393
  837.1 96.5 %copy-start.85 = (f32[154]{0:T(256)S(1)}, f32[154]{0:T(256)}, u32[]{:S(2)}) copy-start(f32[154]{0:T(256)} %copy-done.84) | copy-start | bytes 1852
  837.1 97.9 %copy-start.117 = (f32[154]{0:T(256)S(1)}, f32[154]{0:T(256)}, u32[]{:S(2)}) copy-start(f32[154]{0:T(256)} %copy-done.116) | copy-start | bytes 1852
  837.1 97.9 %copy-start.92 = (f32[154]{0:T(256)S(1)}, f32[154]{0:T(256)}, u32[]{:S(2)}) copy-start(f32[154]{0:T(256)} %copy-done.91) | copy-start | bytes 1852
  837.1 100.1 %copy-start.62 = (f32[1024]{0:T(1024)S(1)}, f32[1024]{0:T(1024)}, u32[]{:S(2)}) copy-start(f32[1024]{0:T(1024)} %copy-done.60) | copy-start | bytes 12292
  966.5 34.1 %copy-start.112 = (f32[1024]{0:T(1024)S(1)}, f32[1024]{0:T(1024)}, u32[]{:S(2)}) copy-start(f32[1024]{0:T(1024)} %get-tuple-element.302) | copy-start | bytes 12292
  (141 other events, 1125.1 us)
Sparse Core Ops, SparseCore 0:
  29.3 33.5 all-reduce.2
Sparse Core Ops, SparseCore 1:
  31.6 47.9 all-gather.6
  81.4 28.7 all-gather.8
  111.9 58.5 all-gather.10
  172.5 58.5 all-gather.12
  622.7 41.5 reduce-scatter.6
  744.7 63.4 reduce-scatter.4
  811.6 76.6 reduce-scatter.10
  891.6 78.9 reduce-scatter.8

commit v2 on v0

v2 whole, which is shorter than its diff:
```python
import functools
import math

import jax
import jax.numpy as jnp
from jax import lax
from jax.experimental import pallas as pl
from jax.experimental.pallas import tpu as pltpu
from jax.sharding import PartitionSpec as P

D = 1536
HEAD_DIM = 64
PAIR = 2 * HEAD_DIM
SUB = 64
F32, BF16 = jnp.float32, jnp.bfloat16
NN = (((1,), (0,)), ((), ()))
NT = (((1,), (1,)), ((), ()))
MESH = pl.DeviceIdType.MESH
ANY = pl.BlockSpec(memory_space=pl.ANY)
VM = pl.BlockSpec(memory_space=pltpu.VMEM)
VMEM_MAX = 67_043_328
DMA = pltpu.SemaphoreType.DMA


def dot(left, right, dims=NN):
    return lax.dot_general(left, right, dims, preferred_element_type=F32)


def time_embed(time_steps, first_col, width_count):
    feature_idx = first_col + jnp.arange(width_count, dtype=jnp.int32)
    half_width = D // 2
    frequency = jnp.exp(
        -math.log(10000.0) * (feature_idx % half_width).astype(jnp.float32) / half_width
    )
    phase_arg = time_steps.astype(jnp.float32)[:, None] * frequency[None, :]
    return jnp.where(feature_idx[None, :] < half_width, jnp.cos(phase_arg), jnp.sin(phase_arg))


def norm_rows(rows):
    center = rows - jnp.mean(rows, axis=-1, keepdims=True)
    rstd = lax.rsqrt(jnp.mean(center * center, axis=-1, keepdims=True) + 1e-06)
    return center * rstd, rstd


def start_of(k, li):
    image_pieces = li // SUB
    if isinstance(k, int):
        if k < image_pieces:
            return k * SUB, SUB
        return li + (k - image_pieces) * 80, 80
    return pl.multiple_of(k * SUB, SUB), SUB


class ZSum:
    def __init__(self, size, li, own, come, total, sems):
        self.li, self.own, self.come, self.total = li, own, come, total
        self.s1, self.s2, self.r1, self.r2, self.r3 = sems
        me = lax.axis_index("tensor")
        half = size // 2
        self.mid = (me == half - 1) | (me == half)
        self.end = jnp.logical_not(self.mid)
        self.inward = jnp.where(me < half, me + 1, me - 1)
        self.outward = jnp.where(me < half, me - 1, me + 1)

    def barrier(self):
        bar = pltpu.get_barrier_semaphore()
        pl.semaphore_signal(bar, inc=1, device_id={"tensor": self.inward}, device_id_type=MESH)

        @pl.when(self.mid)
        def _():
            pl.semaphore_signal(bar, inc=1, device_id={"tensor": self.outward}, device_id_type=MESH)
            pl.semaphore_wait(bar, 2)

        @pl.when(self.end)
        def _():
            pl.semaphore_wait(bar, 1)

    def at(self, k):
        r0, n = start_of(k, self.li)
        return pl.ds(r0, n)

    def _copy(self, src, dst, send, recv, k, where):
        return pltpu.make_async_remote_copy(
            src.at[self.at(k)], dst.at[self.at(k)], send.at[k], recv.at[k],
            device_id={"tensor": where}, device_id_type=MESH,
        )

    def to_mid(self, k):
        return self._copy(self.own, self.come, self.s1, self.r1, k, self.inward)

    def swap(self, k):
        return self._copy(self.own, self.total, self.s1, self.r2, k, self.inward)

    def back(self, k):
        return self._copy(self.total, self.total, self.s2, self.r3, k, self.outward)

    def fold(self, k):
        self.to_mid(k).wait_recv()
        at = self.at(k)
        self.own[at, :] = (self.own[at, :].astype(F32) + self.come[at, :].astype(F32)).astype(BF16)
        self.swap(k).start()

    def close(self, k):
        self.swap(k).wait_recv()
        at = self.at(k)
        self.total[at, :] = (self.own[at, :].astype(F32) + self.total[at, :].astype(F32)).astype(BF16)
        self.back(k).start()

    def drain(self, pieces):
        @pl.when(self.mid)
        def _():
            def go(k, c):
                self.swap(k).wait_send()
                self.back(k).wait_send()
                return c

            lax.fori_loop(0, self.li // SUB, go, 0)
            for k in range(self.li // SUB, pieces):
                go(k, 0)

        @pl.when(self.end)
        def _():
            def go(k, c):
                self.to_mid(k).wait_send()
                return c

            lax.fori_loop(0, self.li // SUB, go, 0)
            for k in range(self.li // SUB, pieces):
                go(k, 0)


def z_scratch(rows, pieces):
    return [pltpu.VMEM((rows, D), BF16)] * 2 + [DMA((pieces,))] * 5


def ln_kernel(li, x_ref, mod_ref, o_ref):
    def block(r0, n, s):
        m, _ = norm_rows(x_ref[pl.ds(r0, n), :].astype(F32))
        o_ref[pl.ds(r0, n), :] = (m * (1.0 + mod_ref[6 * s + 1 : 6 * s + 2, :]) + mod_ref[6 * s : 6 * s + 1, :]).astype(BF16)

    def body(i, c):
        block(pl.multiple_of(i * 64, 64), 64, 0)
        return c

    lax.fori_loop(0, li // 64, body, 0)
    block(li, x_ref.shape[0] - li, 1)


def ln_call(x, mod, li):
    return pl.pallas_call(
        functools.partial(ln_kernel, li),
        out_shape=jax.ShapeDtypeStruct(x.shape, BF16),
        in_specs=[VM, VM],
        out_specs=VM,
        compiler_params=pltpu.CompilerParams(vmem_limit_bytes=24 << 20),
    )(x, mod)


def half_lanes(rows, low):
    lane = lax.broadcasted_iota(jnp.int32, rows.shape, 1)
    return jnp.where((lane < HEAD_DIM) == low, rows, jnp.zeros_like(rows))


def qkv_attend_kernel(
    size, li, valid, n_ref, w_ref, b_ref, qkv_ref, o_ref, total, own, come, km, vm, *sems
):
    rows, width = qkv_ref.shape
    cols = width // 3
    z = ZSum(size, li, own, come, total, sems)
    image_pieces = li // SUB
    text = (image_pieces, image_pieces + 1)
    step, per, lag = 256, 256 // SUB, 2
    z.barrier()

    def project(r0, n, s):
        got = dot(n_ref[pl.ds(r0, n), :], w_ref[s, :, :width]) + b_ref[s : s + 1, :]
        qkv_ref[pl.ds(r0, n), :] = got.astype(BF16)

    def project_image(i, c):
        project(pl.multiple_of(i * step, step), step, 0)
        return c

    project(li, rows - li, 1)
    lax.fori_loop(0, li // step, project_image, 0)

    def lanes(j, p):
        return slice(j * cols + p * PAIR, j * cols + (p + 1) * PAIR)

    pairs = cols // PAIR
    for p in range(pairs):
        for h in range(2):
            km[2 * p + h] = half_lanes(qkv_ref[:, lanes(1, p)], h == 0)
            vm[2 * p + h] = half_lanes(qkv_ref[:, lanes(2, p)], h == 0)

    def block(r0, n, s):
        at = pl.ds(r0, n)
        for p in range(pairs):
            q2 = qkv_ref[at, lanes(0, p)]
            mixed = 0.0
            for h in range(2):
                scores = dot(q2, km[2 * p + h], NT)
                col = lax.broadcasted_iota(jnp.int32, scores.shape, 1)
                scores = jnp.where(col < valid, scores, -1e30)
                e = jnp.exp((scores - jnp.max(scores, axis=1, keepdims=True)) * HEAD_DIM**-0.5)
                norm = 1.0 / jnp.sum(e, axis=1, keepdims=True)
                mixed = mixed + dot(e.astype(BF16), vm[2 * p + h]) * norm
            o_ref[at, lanes(0, p)] = mixed.astype(BF16)
        own[at, :] = dot(o_ref[at, :], w_ref[s, :, width:], NT).astype(BF16)

    block(li, rows - li, 1)

    @pl.when(z.end)
    def _():
        for k in text:
            z.to_mid(k).start()

    def image_block(i, c):
        block(pl.multiple_of(i * step, step), step, 0)

        @pl.when(z.end)
        def _():
            for j in range(per):
                z.to_mid(i * per + j).start()

        @pl.when(z.mid & (i == 0))
        def _():
            for k in text:
                z.fold(k)

        @pl.when(z.mid & (i >= 1))
        def _():
            for j in range(per):
                k = (i - 1) * per + j
                z.fold(k)
                if j >= lag:
                    z.close(k - lag)
                else:
                    @pl.when(i == 1)
                    def _():
                        z.close(text[j])

                    @pl.when(i >= 2)
                    def _():
                        z.close(k - lag)

        return c

    lax.fori_loop(0, li // step, image_block, 0)

    @pl.when(z.mid)
    def _():
        for k in range(image_pieces - per, image_pieces):
            z.fold(k)
            z.close(k - lag)
        for k in range(image_pieces - lag, image_pieces):
            z.close(k)

    @pl.when(z.end)
    def _():
        def go(k, c):
            z.back(k).wait_recv()
            return c

        lax.fori_loop(0, image_pieces, go, 0)
        for k in text:
            go(k, 0)

    z.drain(image_pieces + 2)


def qkv_attend_call(normed, weight, bias, size, li, valid, cid):
    rows, width = normed.shape[0], bias.shape[1]
    pieces = li // SUB + 2
    shape = jax.ShapeDtypeStruct
    heads = width // 3 // HEAD_DIM
    return pl.pallas_call(
        functools.partial(qkv_attend_kernel, size, li, valid),
        out_shape=[shape((rows, width), BF16), shape((rows, width // 3), BF16), shape((rows, D), BF16)],
        in_specs=[VM] * 3,
        out_specs=[VM] * 3,
        scratch_shapes=[
            pltpu.VMEM((rows, D), BF16), pltpu.VMEM((rows, D), BF16),
            pltpu.VMEM((heads, rows, PAIR), BF16), pltpu.VMEM((heads, rows, PAIR), BF16),
        ] + [DMA((pieces,))] * 5,
        compiler_params=pltpu.CompilerParams(
            collective_id=cid, has_side_effects=True, vmem_limit_bytes=60 << 20
        ),
    )(normed, weight, bias)


def grads_kernel(li, groups, *refs):
    out = refs[-1]
    at = 0
    for left, right, gate in groups:
        l_ref, r_ref = refs[left], refs[right]
        n = r_ref.shape[1]
        for s in (0, 1):
            span = slice(0, li) if s == 0 else slice(li, l_ref.shape[0])
            lhs = l_ref[span, :]
            if gate is not None:
                g_ref, row = refs[gate[0]], 6 * s + gate[1]
                lhs = (g_ref[row : row + 1, :] * lhs.astype(F32)).astype(BF16)
            got = lax.dot_general(lhs, r_ref[span, :], (((0,), (0,)), ((), ())), preferred_element_type=F32)
            out[:, at : at + n] = got.astype(BF16)
            at += n


def grads_call(pairs, mod, li):
    block = 256
    args, specs, groups = [], [], []
    total = 0
    for left, right, gated in pairs:
        rows = left.shape[0]
        args += [left, right]
        specs += [
            pl.BlockSpec((rows, block), lambda i: (0, i)),
            pl.BlockSpec(right.shape, lambda i: (0, 0), pipeline_mode=pl.Buffered(1)),
        ]
        groups.append((len(args) - 2, len(args) - 1, gated))
        total += 2 * right.shape[1]
    if any(gated for _, _, gated in pairs):
        args.append(mod)
        specs.append(pl.BlockSpec((mod.shape[0], block), lambda i: (0, i)))
    groups = [(l, r, (len(args) - 1, 5) if gated else None) for l, r, gated in groups]
    return pl.pallas_call(
        functools.partial(grads_kernel, li, groups),
        grid=(D // block,),
        out_shape=jax.ShapeDtypeStruct((D, total), BF16),
        in_specs=specs,
        out_specs=pl.BlockSpec((block, total), lambda i: (i, 0)),
        compiler_params=pltpu.CompilerParams(vmem_limit_bytes=60 << 20),
    )(*args)


def proj_sum_kernel(size, li, dims, x_ref, w_ref, total, own, come, *sems):
    rows = x_ref.shape[0]
    z = ZSum(size, li, own, come, total, sems)
    image_pieces = li // SUB
    pieces = image_pieces + 2
    z.barrier()
    step = 256

    def project(r0, n, s):
        own[pl.ds(r0, n), :] = dot(x_ref[pl.ds(r0, n), :], w_ref[s, :, : x_ref.shape[1]], dims).astype(BF16)

    project(li, rows - li, 1)

    @pl.when(z.end)
    def _():
        for k in range(image_pieces, pieces):
            z.to_mid(k).start()

    def image_block(i, c):
        project(pl.multiple_of(i * step, step), step, 0)

        @pl.when(z.end)
        def _():
            for j in range(step // SUB):
                z.to_mid(i * (step // SUB) + j).start()

        return c

    lax.fori_loop(0, li // step, image_block, 0)
    first, second = image_pieces, image_pieces + 1

    @pl.when(z.mid)
    def _():
        lag = 2
        for k in (first, second):
            z.fold(k)
        for k in range(lag):
            z.fold(k)
        z.close(first)
        z.close(second)

        def go(k, c):
            z.fold(k)
            z.close(k - lag)
            return c

        lax.fori_loop(lag, image_pieces, go, 0)
        for k in range(image_pieces - lag, image_pieces):
            z.close(k)

    @pl.when(z.end)
    def _():
        def go(k, c):
            z.back(k).wait_recv()
            return c

        lax.fori_loop(0, image_pieces, go, 0)
        go(first, 0)
        go(second, 0)

    z.drain(pieces)


def proj_sum_call(x, w, size, li, dims, cid):
    rows = x.shape[0]
    pieces = li // SUB + 2
    return pl.pallas_call(
        functools.partial(proj_sum_kernel, size, li, dims),
        out_shape=jax.ShapeDtypeStruct((rows, D), BF16),
        in_specs=[VM] * 2,
        out_specs=VM,
        scratch_shapes=z_scratch(rows, pieces),
        compiler_params=pltpu.CompilerParams(
            collective_id=cid, has_side_effects=True, vmem_limit_bytes=48 << 20
        ),
    )(x, w)


ROOT_2_PI = math.sqrt(2.0 / math.pi)


def gelu_and_slope(x):
    square = x * x
    t = jnp.tanh(ROOT_2_PI * x * (1.0 + 0.044715 * square))
    half = 0.5 * (1.0 + t)
    slope = half + 0.5 * x * (1.0 - t * t) * (ROOT_2_PI * (1.0 + 3 * 0.044715 * square))
    return x * half, slope


def mlp_kernel(
    size, li,
    a_ref, x_hbm, g_hbm, w_hbm, wo_hbm, mod_ref, ob_ref, ib_ref,
    n2_hbm, act_hbm, du_hbm, pm_hbm, dr_hbm, da_hbm, dmix_ref, sums_ref,
    xv, gv, wi, wm, wo_ref, own, come, total, st_n2, st_act, st_du, st_pm, st_dr, st_da, load, put, *sems,
):
    rows = a_ref.shape[0]
    hid, cols = wi.shape[2], wo_ref.shape[2]
    z = ZSum(size, li, own, come, total, sems)
    chunk = 2 * SUB
    chunks = li // chunk
    lt = rows - li
    text = (li // SUB, li // SUB + 1)
    loads = [
        pltpu.make_async_copy(x_hbm, xv, load.at[0]),
        pltpu.make_async_copy(g_hbm, gv, load.at[1]),
        pltpu.make_async_copy(w_hbm.at[1, :, pl.ds(0, hid)], wi.at[1], load.at[2]),
        pltpu.make_async_copy(w_hbm.at[1, :, pl.ds(hid, hid)], wm.at[1], load.at[3]),
        pltpu.make_async_copy(w_hbm.at[0, :, pl.ds(0, hid)], wi.at[0], load.at[4]),
        pltpu.make_async_copy(w_hbm.at[0, :, pl.ds(hid, hid)], wm.at[0], load.at[5]),
        pltpu.make_async_copy(wo_hbm.at[:, :, pl.ds(3 * cols, cols)], wo_ref, load.at[6]),
    ]
    for copy in loads:
        copy.start()
    z.barrier()
    sums_ref[...] = jnp.zeros_like(sums_ref)
    outs = ((st_n2, n2_hbm), (st_act, act_hbm), (st_du, du_hbm), (st_pm, pm_hbm), (st_dr, dr_hbm), (st_da, da_hbm))

    def store(j, r0, n, slot):
        stage, hbm = outs[j]
        return pltpu.make_async_copy(
            stage.at[slot, pl.ds(0, n), :], hbm.at[pl.ds(r0, n), :], put.at[j, slot]
        )

    def resid_of(at, s):
        branch = a_ref[at, :].astype(F32) + ob_ref[s : s + 1, :]
        resid = xv[at, :].astype(F32) + mod_ref[6 * s + 2 : 6 * s + 3, :] * branch
        m, rstd = norm_rows(resid)
        return branch, m, rstd

    def add_sum(s, j, value):
        sums_ref[8 * s + j : 8 * s + j + 1, :] += jnp.sum(value, axis=0, keepdims=True)

    def forward(r0, n, s, slot):
        at = pl.ds(r0, n)
        _, m, _ = resid_of(at, s)
        st_n2[slot, :n, :] = (m * (1.0 + mod_ref[6 * s + 4 : 6 * s + 5, :]) + mod_ref[6 * s + 3 : 6 * s + 4, :]).astype(BF16)
        d_mlp = mod_ref[6 * s + 5 : 6 * s + 6, :] * gv[at, :].astype(F32)
        add_sum(s, 5, d_mlp)
        d_mlp = d_mlp.astype(BF16)
        width = 512
        for j in range(hid // width):
            cols = slice(j * width, (j + 1) * width)
            upper = dot(st_n2[slot, :n, :], wi[s, :, cols]) + ib_ref[s : s + 1, cols]
            act, slope = gelu_and_slope(upper)
            st_act[slot, :n, cols] = act.astype(BF16)
            d_upper = (dot(d_mlp, wm[s, :, cols]) * slope).astype(BF16)
            st_du[slot, :n, cols] = d_upper
            sums_ref[8 * s + 4 : 8 * s + 5, cols] += jnp.sum(d_upper.astype(F32), axis=0, keepdims=True)
        own[at, :] = dot(st_du[slot, :n, :], wi[s], NT).astype(BF16)
        for k in (0, 1, 2):
            store(k, r0, n, slot).start()

    def partial(r0, n, s, slot):
        st_pm[slot, :n, :] = dot(st_act[slot, :n, :], wm[s], NT).astype(BF16)
        store(3, r0, n, slot).start()

    def backward(r0, n, s, slot):
        at = pl.ds(r0, n)
        branch, m, rstd = resid_of(at, s)
        d_mid = total[at, :].astype(F32)
        add_sum(s, 0, d_mid)
        add_sum(s, 1, d_mid * m)
        e = d_mid * (1.0 + mod_ref[6 * s + 4 : 6 * s + 5, :])
        back = (e - jnp.mean(e, axis=-1, keepdims=True) - m * jnp.mean(e * m, axis=-1, keepdims=True)) * rstd
        d_resid = back + gv[at, :].astype(F32)
        st_dr[slot, :n, :] = d_resid
        add_sum(s, 2, d_resid * branch)
        d_attn = mod_ref[6 * s + 2 : 6 * s + 3, :] * d_resid
        add_sum(s, 3, d_attn)
        low = d_attn.astype(BF16)
        st_da[slot, :n, :] = low
        dmix_ref[at, :] = dot(low, wo_ref[s]).astype(BF16)
        for k in (4, 5):
            store(k, r0, n, slot).start()

    for j in (0, 1, 2, 3):
        loads[j].wait()
    forward(li, lt, 1, 2)

    @pl.when(z.end)
    def _():
        for k in text:
            z.to_mid(k).start()

    partial(li, lt, 1, 2)
    for j in (4, 5, 6):
        loads[j].wait()

    def at_chunk(i):
        return pl.multiple_of(i * chunk, chunk)

    def step(i, c):
        slot = lax.rem(i, 2)

        @pl.when((i >= 2) & (i < chunks))
        def _():
            for j in (0, 1, 2, 3):
                store(j, at_chunk(i - 2), chunk, slot).wait()

        @pl.when(i < chunks)
        def _():
            forward(at_chunk(i), chunk, 0, slot)

            @pl.when(z.end)
            def _():
                z.to_mid(2 * i).start()
                z.to_mid(2 * i + 1).start()

            partial(at_chunk(i), chunk, 0, slot)

        @pl.when(z.mid & (i == 0))
        def _():
            for k in text:
                z.fold(k)

        @pl.when(z.mid & (i >= 1) & (i <= chunks))
        def _():
            z.fold(2 * (i - 1))
            z.fold(2 * (i - 1) + 1)

        @pl.when(z.mid & (i == 1))
        def _():
            for k in text:
                z.close(k)

        @pl.when(z.mid & (i >= 2) & (i <= chunks + 1))
        def _():
            z.close(2 * (i - 2))
            z.close(2 * (i - 2) + 1)

        @pl.when(i >= 5)
        def _():
            for j in (4, 5):
                store(j, at_chunk(i - 5), chunk, lax.rem(i - 3, 2)).wait()

        @pl.when(i >= 3)
        def _():
            @pl.when(z.end)
            def _():
                z.back(2 * (i - 3)).wait_recv()
                z.back(2 * (i - 3) + 1).wait_recv()

            backward(at_chunk(i - 3), chunk, 0, lax.rem(i - 3, 2))

        return c

    lax.fori_loop(0, chunks + 3, step, 0)

    @pl.when(z.end)
    def _():
        for k in text:
            z.back(k).wait_recv()

    backward(li, lt, 1, 2)
    for j in range(6):
        store(j, li, lt, 2).wait()
        for i in (chunks - 2, chunks - 1):
            store(j, i * chunk, chunk, i % 2).wait()
    z.drain(len(text) + li // SUB)


def mlp_call(a, x, g, w, wo, mod, ob, ib, cols, size, li, cid):
    rows, hid = a.shape[0], ib.shape[1]
    pieces = li // SUB + 2
    lt = rows - li
    shape = jax.ShapeDtypeStruct
    tall = max(lt, 2 * SUB)
    return pl.pallas_call(
        functools.partial(mlp_kernel, size, li),
        out_shape=[
            shape((rows, D), BF16), shape((rows, hid), BF16), shape((rows, hid), BF16), shape((rows, D), BF16),
            shape((rows, D), F32), shape((rows, D), BF16), shape((rows, cols), BF16), shape((16, D), F32),
        ],
        in_specs=[VM, ANY, ANY, ANY, ANY, VM, VM, VM],
        out_specs=[ANY] * 6 + [VM] * 2,
        scratch_shapes=[
            pltpu.VMEM((rows, D), BF16), pltpu.VMEM((rows, D), BF16),
            pltpu.VMEM((2, D, hid), BF16), pltpu.VMEM((2, D, hid), BF16), pltpu.VMEM((2, D, cols), BF16),
            pltpu.VMEM((rows, D), BF16), pltpu.VMEM((rows, D), BF16), pltpu.VMEM((rows, D), BF16),
            pltpu.VMEM((3, tall, D), BF16), pltpu.VMEM((3, tall, hid), BF16), pltpu.VMEM((3, tall, hid), BF16),
            pltpu.VMEM((3, tall, D), BF16), pltpu.VMEM((3, tall, D), F32), pltpu.VMEM((3, tall, D), BF16),
            DMA((7,)), DMA((6, 3)),
        ] + [DMA((pieces,))] * 5,
        compiler_params=pltpu.CompilerParams(
            collective_id=cid, has_side_effects=True, vmem_limit_bytes=VMEM_MAX
        ),
    )(a, x, g, w, wo, mod, ob, ib)


def attend_back_kernel(
    size, li, valid, qkv_ref, do_ref, pm_hbm, d_ref, total, own, come, dk_acc, dv_acc, kt, load, *sems
):
    rows, width = qkv_ref.shape
    cols = width // 3
    z = ZSum(size, li, own, come, total, sems)
    image_pieces = li // SUB
    text = (image_pieces, image_pieces + 1)
    fetch = pltpu.make_async_copy(pm_hbm, own, load)
    fetch.start()
    z.barrier()
    fetch.wait()

    @pl.when(z.end)
    def _():
        for k in text:
            z.to_mid(k).start()

        def go(k, c):
            z.to_mid(k).start()
            return c

        lax.fori_loop(0, image_pieces, go, 0)

    lag = 2
    per_pair = li // 256

    def tick(k):
        @pl.when(z.mid & (k < image_pieces))
        def _():
            z.fold(k)

        @pl.when(z.mid & (k >= lag) & (k < image_pieces + lag))
        def _():
            z.close(k - lag)

    for p in range(cols // PAIR):
        at = lambda j: slice(j * cols + p * PAIR, j * cols + (p + 1) * PAIR)
        k2, v2 = qkv_ref[:, at(1)], qkv_ref[:, at(2)]
        kt[...] = k2.astype(F32).T.astype(BF16)
        ks = [half_lanes(k2, low) for low in (True, False)]
        vs = [half_lanes(v2, low) for low in (True, False)]
        dk_acc[...] = jnp.zeros_like(dk_acc)
        dv_acc[...] = jnp.zeros_like(dv_acc)

        def block(r0, n):
            q2 = qkv_ref[pl.ds(r0, n), at(0)]
            g2 = do_ref[pl.ds(r0, n), at(0)]
            parts = []
            for h in range(2):
                s = dot(ks[h], q2, NT)
                row = lax.broadcasted_iota(jnp.int32, s.shape, 0)
                s = jnp.where(row < valid, s, -1e30)
                e = jnp.exp((s - jnp.max(s, axis=0, keepdims=True)) * HEAD_DIM**-0.5)
                probs = e * (1.0 / jnp.sum(e, axis=0, keepdims=True))
                d_probs = dot(vs[h], g2, NT)
                delta = jnp.sum(probs * d_probs, axis=0, keepdims=True)
                ds = (probs * (d_probs - delta)).astype(BF16)
                dk_acc[...] += dot(ds, half_lanes(q2, h == 0))
                dv_acc[...] += dot(probs.astype(BF16), half_lanes(g2, h == 0))
                parts.append(dot(kt[h * HEAD_DIM : (h + 1) * HEAD_DIM, :], ds))
            d_q = jnp.concatenate(parts, axis=0).T * HEAD_DIM**-0.5
            d_ref[pl.ds(r0, n), at(0)] = d_q.astype(BF16)

        if p == 0:
            block(li, rows - li)

            @pl.when(z.mid)
            def _():
                for k in text:
                    z.fold(k)

        def image_block(i, c):
            block(pl.multiple_of(i * 256, 256), 256)
            tick(p * (per_pair + 1) + i)
            return c

        lax.fori_loop(0, per_pair, image_block, 0)
        if p == 0:
            @pl.when(z.mid)
            def _():
                for k in text:
                    z.close(k)
        else:
            block(li, rows - li)
        at_end = p * (per_pair + 1) + per_pair

        @pl.when(z.mid)
        def _():
            z.fold(at_end)
            z.close(at_end - lag)

        d_ref[:, at(1)] = (dk_acc[...] * HEAD_DIM**-0.5).astype(BF16)
        d_ref[:, at(2)] = dv_acc[...].astype(BF16)

    def rest(k, c):
        tick(k)
        return c

    lax.fori_loop((cols // PAIR) * (per_pair + 1), image_pieces + lag, rest, 0)

    @pl.when(z.end)
    def _():
        def go(k, c):
            z.back(k).wait_recv()
            return c

        lax.fori_loop(0, image_pieces, go, 0)
        for k in text:
            go(k, 0)

    z.drain(image_pieces + 2)


def attend_back_call(qkv, d_mix, pm, size, li, valid, cid):
    rows, width = qkv.shape
    pieces = li // SUB + 2
    return pl.pallas_call(
        functools.partial(attend_back_kernel, size, li, valid),
        out_shape=[jax.ShapeDtypeStruct((rows, width), BF16), jax.ShapeDtypeStruct((rows, D), BF16)],
        in_specs=[VM, VM, ANY],
        out_specs=[VM, VM],
        scratch_shapes=[
            pltpu.VMEM((rows, D), BF16), pltpu.VMEM((rows, D), BF16),
            pltpu.VMEM((rows, PAIR), F32), pltpu.VMEM((rows, PAIR), F32), pltpu.VMEM((PAIR, rows), BF16), DMA,
        ] + [DMA((pieces,))] * 5,
        compiler_params=pltpu.CompilerParams(
            collective_id=cid, has_side_effects=True, vmem_limit_bytes=60 << 20
        ),
    )(qkv, d_mix, pm)


def shards(
    image, text, pooled, timestep, grad_image, grad_text, ada_weight, ada_bias, qkv_weight, qv_bias,
    out_weight, out_bias, mlp_in_weight, mlp_in_bias, mlp_out_weight, mlp_out_bias,
):
    size = lax.axis_size("tensor")
    li, lt = image.shape[1], text.shape[1]
    pad = -lt % 16
    spans = (slice(0, li), slice(li, li + lt + pad))
    valid = li + lt
    cols = out_weight.shape[1]

    def joint(image_rows, text_rows):
        return jnp.concatenate([image_rows[0], jnp.pad(text_rows[0], ((0, pad), (0, 0)))])

    def gather(weight):
        return lax.all_gather(weight, "dp", axis=1, tiled=True)

    x, g = joint(image, text), joint(grad_image, grad_text)
    packed = jnp.concatenate(
        [qkv_weight.reshape(2, qkv_weight.shape[1], -1), jnp.swapaxes(out_weight, 1, 2)], axis=2
    )
    packed, pooled = lax.optimization_barrier((packed, pooled))
    w_attn = gather(packed)
    w_mlp = gather(jnp.concatenate([mlp_in_weight, jnp.swapaxes(mlp_out_weight, 1, 2)], axis=2))

    width_local = pooled.shape[1]
    first_col = lax.axis_index("tensor") * width_local
    condition = pooled.astype(F32) + time_embed(timestep, first_col, width_local)
    cond_act, silu_pull = jax.vjp(jax.nn.silu, condition)
    cond_all = lax.all_gather(cond_act.astype(BF16), "dp", axis=0, tiled=True)
    mod_part = jnp.einsum("sc,nce->nse", cond_all, ada_weight, preferred_element_type=F32)
    mod_part = lax.all_to_all(mod_part, "dp", split_axis=1, concat_axis=2, tiled=True)
    modul = lax.psum(mod_part, "tensor") + ada_bias.astype(F32)[:, None, :]
    mod = modul.reshape(12, D)

    out_b, in_b, last_b = out_bias.astype(F32), mlp_in_bias.astype(F32), mlp_out_bias.astype(F32)
    qkv_b = jnp.stack([qv_bias[:, 0], jnp.zeros_like(qv_bias[:, 0]), qv_bias[:, 1]], axis=1)
    qkv_b = qkv_b.reshape(2, -1).astype(F32)

    normed = ln_call(x, mod, li)
    qkv, mixed, attn = qkv_attend_call(normed, w_attn, qkv_b, size, li, valid, 1)
    normed2, act, d_upper, mlp_part, d_resid, d_attn, d_mix, sums = mlp_call(
        attn, x, g, w_mlp, w_attn, mod, out_b, in_b, cols, size, li, 2
    )

    def scatter(grad):
        return lax.psum_scatter(grad, "dp", scatter_dimension=0, tiled=True).astype(F32)

    hid = mlp_in_bias.shape[1]
    mlp_grads = grads_call([(normed2, d_upper, False), (g, act, True)], mod, li)
    mlp_grads, mlp_part = lax.optimization_barrier((mlp_grads, mlp_part))
    mlp_shard = scatter(mlp_grads)
    w_in_grad = jnp.stack([mlp_shard[:, :hid], mlp_shard[:, hid : 2 * hid]])
    w_mlp_grad = jnp.stack([mlp_shard[:, 2 * hid : 3 * hid].T, mlp_shard[:, 3 * hid :].T])

    d_qkv, mlp = attend_back_call(qkv, d_mix, mlp_part, size, li, valid, 3)
    attn_grads = grads_call([(d_attn, mixed, False), (normed, d_qkv, False)], mod, li)
    attn_grads, d_qkv = lax.optimization_barrier((attn_grads, d_qkv))
    attn_shard = scatter(attn_grads)
    w_out_grad = jnp.stack([attn_shard[:, :cols].T, attn_shard[:, cols : 2 * cols].T])
    qkv_grad = jnp.stack([attn_shard[:, 2 * cols : 5 * cols], attn_shard[:, 5 * cols :]])
    d_in = proj_sum_call(d_qkv, w_attn, size, li, NT, 4)

    blocks, token_grads, d_mods = [], [], []
    for s in (0, 1):
        rows = slice(0, li) if s == 0 else slice(li, li + lt)
        xs, gs = x[rows].astype(F32), g[rows].astype(F32)
        second = mlp[rows].astype(F32) + last_b[s]
        resid = xs + mod[6 * s + 2] * (attn[rows].astype(F32) + out_b[s])
        blocks.append((resid + mod[6 * s + 5] * second).astype(BF16)[None])
        d_gate2 = jnp.sum(gs * second, axis=0)
        m, rstd = norm_rows(xs)
        d = d_in[rows].astype(F32)
        d_shift, d_scale = jnp.sum(d, axis=0), jnp.sum(d * m, axis=0)
        e = d * (1.0 + mod[6 * s + 1])
        back = (e - jnp.mean(e, axis=-1, keepdims=True) - m * jnp.mean(e * m, axis=-1, keepdims=True)) * rstd
        token_grads.append((d_resid[rows] + back)[None])
        d_mods += [d_shift, d_scale, sums[8 * s + 2], sums[8 * s], sums[8 * s + 1], d_gate2]
    pair = [jnp.sum(d_qkv[spans[s], j * cols : (j + 1) * cols].astype(F32), axis=0) for s in (0, 1) for j in (0, 2)]

    small = d_mods + pair + [sums[8 * s + 3] for s in (0, 1)] + [sums[8 * s + 4] for s in (0, 1)] + [sums[8 * s + 5] for s in (0, 1)]
    every = lax.all_gather(jnp.concatenate(small).astype(BF16), "dp")
    summed = jnp.sum(every.astype(F32), axis=0)
    at = [0]
    for width in (12 * D, 4 * cols, 2 * D, 2 * hid, 2 * D):
        at.append(at[-1] + width)
    pieces = [summed[a:b] for a, b in zip(at, at[1:])]
    ada_cols = ada_weight.shape[2]
    d_mod_cols = lax.dynamic_slice_in_dim(
        every[:, : at[1]].reshape(-1, 2, 6 * D), lax.axis_index("dp") * ada_cols, ada_cols, axis=2
    )
    ada_grad = jnp.einsum("sc,sne->nce", cond_all, d_mod_cols, preferred_element_type=F32)
    d_cond_act = lax.psum_scatter(
        jnp.einsum("sne,nce->sc", d_mod_cols, ada_weight, preferred_element_type=F32),
        "dp", scatter_dimension=0, tiled=True,
    )
    (pooled_grad,) = silu_pull(d_cond_act)
    return (
        blocks[0],
        blocks[1],
        token_grads[0],
        token_grads[1],
        pooled_grad,
        ada_grad,
        pieces[0].reshape(2, 6 * D),
        qkv_grad.reshape(2, -1, 3, cols),
        pieces[1].reshape(2, 2, cols),
        w_out_grad,
        pieces[2].reshape(2, D),
        w_in_grad,
        pieces[3].reshape(2, hid),
        w_mlp_grad,
        pieces[4].reshape(2, D),
    )


def solution(mesh):
    t = "tensor"
    rows, last, mid = P("dp", None, None), P(None, t, "dp"), P(None, "dp", t)
    return jax.shard_map(
        shards,
        mesh=mesh,
        in_specs=(
            rows, rows, P("dp", t), P("dp"), rows, rows, last, P(), P(None, "dp", None, t), P(None, None, t),
            last, P(), mid, P(None, t), last, P(),
        ),
        out_specs=(
            rows, rows, rows, rows, P("dp", t), last, P(), P(None, "dp", None, t), P(None, None, t),
            last, P(), mid, P(None, t), last, P(),
        ),
        check_vma=False,
    )
```

time: 1540 us -> 699 us (0.45)
  waiting for transfers between devices: 954 us -> 55.7 us
  Pallas kernels: 0 us -> 480 us
  matrix products: 229 us -> 3.2 us
  other arithmetic: 164 us -> 51.4 us
  local copies, waits for them, and re-layouts: 136 us -> 23.4 us
  blocking collectives: 23.7 us -> 58.5 us
    pallas_call x0 -> x7, Pallas kernels: none -> 480 us  [the longest x1 116 us: mlp_call(): pl.pallas_call(functools.partial(mlp_kernel, size, li), out_shape=[shape(...]
    psum x4 -> x1, waiting for transfers between devices: 442 us -> 22.3 us  [shards(): modul = lax.psum(mod_part, 'tensor') + ada_bias.astype(F32)[:, None, :]]
    dot_general x41 -> x3, matrix products: 229 us -> 3.2 us  [the longest x1 2.19 us: shards(): jnp.einsum('sne,nce->sc', d_mod_cols, ada_weight, preferred_element_type=...]
    all_gather x5 -> x2, waiting for transfers between devices: 231 us -> 18 us  [gather(): return lax.all_gather(weight, 'dp', axis=1, tiled=True)]
    unnamed x15 -> x5, waiting for transfers between devices: 181 us -> 1.25 us
    reduce_scatter x2, waiting for transfers between devices: 100 us -> 14.2 us  [scatter(): lax.psum_scatter(grad, 'dp', scatter_dimension=0, tiled=True).astype(F32)]
    unnamed x244 -> x84, local copies, waits for them, and re-layouts: 67.6 us -> 13.7 us
    reduce_sum x24 -> x13, other arithmetic: 76.8 us -> 28.5 us  [the longest x2 15.2 us: shards(): d_gate2 = jnp.sum(gs * second, axis=0)]
  transfers between devices with their start and end apart: 13 -> 5, of which waited for: 12 -> 3; matrix products, arithmetic and copies ran while one was open for 22% -> 9% of each run, Pallas kernels for 0% -> 32%
where the time goes in v2:
time: 699 us; the launch traced here: 690 us
  Pallas kernels  480 us (69%)
  blocking collectives  58.5 us (8%)
  waiting for transfers between devices  55.7 us (8%)
  other arithmetic  51.4 us (7%)
  local copies, waits for them, and re-layouts  23.4 us (3%)
  between operations  17.4 us (2%)
    pallas_call x1, Pallas kernels, mlp_call(): pl.pallas_call(functools.partial(mlp_kernel, size, li), out_shape=[shape(...  116 us
    pallas_call x1, Pallas kernels, qkv_attend_call(): pl.pallas_call(functools.partial(qkv_attend_kernel, size, li, valid), out...  115 us
    pallas_call x1, Pallas kernels, attend_back_call(): pl.pallas_call(functools.partial(attend_back_kernel, size, li, valid), ou...  110 us
    pallas_call x1, Pallas kernels, proj_sum_call(): pl.pallas_call(functools.partial(proj_sum_kernel, size, li, dims), out_sh...  102 us
    pallas_call x2, Pallas kernels, grads_call(): pl.pallas_call(functools.partial(grads_kernel, li, groups), grid=(D // bl...  32.2 us
    unnamed x1, blocking collectives  24.5 us
    psum x1, waiting for transfers between devices, shards(): modul = lax.psum(mod_part, 'tensor') + ada_bias.astype(F32)[:, None, :]  22.3 us
    all_gather x2, waiting for transfers between devices, gather(): return lax.all_gather(weight, 'dp', axis=1, tiled=True)  18 us
  transfers between devices with their start and end apart: 5, of which 3 were waited for; matrix products, arithmetic and copies ran while one was open for 9% of the time, Pallas kernels for 32%

profile of v2, /device:TPU:0, one launch (start us, length us, event | category | flops | bytes accessed | tf_op | source)
XLA Modules:
  0.0 689.9 jit_solution(10668497497109018712)
XLA Ops:
  9.5 2.1 pad_maximum_fusion.4
  12.9 10.4 %all-gather = bf16[8,1,384]{2,1,0:T(2,128)(2,1)S(1)} all-gather(bf16[1,1,384]{2,1,0:T(2,128)(2,1)S(1)} %get-tuple-element.135), channel_id=1, replica_groups=mesh['dp'=8,'tensor'=4] {'dp'}, dimensions={0}, use_global_device_ids=true | all-gather | bytes 6912 | tf_op jit(solution)/shard_map/all_gather | solution.py:785
  23.7 8.1 %all_to_all.12 = f32[2,8,1152]{2,0,1:T(2,128)} all-to-all(f32[2,8,1152]{2,0,1:T(2,128)S(1)} %copy.46), channel_id=1, replica_groups=mesh['dp'=8,'tensor'=4] {'dp'}, dimensions={1} | all-to-all | bytes 147456 | tf_op jit(solution)/shard_map/all_to_all | solution.py:787
  32.5 3.4 pad_maximum_fusion
  38.0 5.2 fusion.17
  43.2 22.3 %all-reduce.5.cloned.1.call-done = f32[2,1,9216]{2,0,1:T(2,128)} async-done(((f32[2,1,9216]{2,0,1:T(2,128)}), f32[2,1,9216]{2,0,1:T(2,128)}) %all-reduce.5.cloned.1.call-update) | async-done | bytes 73744 | tf_op jit(solution)/shard_map/psum | solution.py:788
  66.6 2.1 copy-done
  68.6 4.3 shard_map.271.n_ref.refs_2_
  73.0 1.8 copy-done.1
  74.8 17.9 %all-gather.5.cloned.1.call-done.w_ref.wo_hbm = bf16[2,1536,1536]{2,1,0:T(8,128)(2,1)} async-done(((bf16[2,192,1536]{2,1,0:T(8,128)(2,1)}), bf16[2,1536,1536]{2,1,0:T(8,128)(2,1)}) %all-gather.5.cloned.1.call-update) | async-done | bytes 9437200 | tf_op jit(solution)/shard_map/all_gather | solution.py:771
  92.7 115.1 %shard_map.272 = (bf16[1184,1152]{1,0:T(8,128)(2,1)}, bf16[1184,384]{1,0:T(8,128)(2,1)}, bf16[1184,1536]{1,0:T(8,128)(2,1)}) custom-call(bf16[1184,1536]{1,0:T(8,128)(2,1)} %copy-done.1, bf16[2,1536,1536]{2,1,0:T(8,128)(2,1)} %all-gather.5.cloned.1.call-done.w_ref.wo_hbm, f32[2,1152]{1,0:T(2,128)} %bitcast.94), custom_call_target="tpu_custom_call" | custom-call | tf_op jit(solution)/shard_map/pallas_call | solution.py:276
  207.9 115.7 %shard_map.273 = (bf16[1184,1536]{1,0:T(8,128)(2,1)}, bf16[1184,1536]{1,0:T(8,128)(2,1)}, bf16[1184,1536]{1,0:T(8,128)(2,1)}, bf16[1184,1536]{1,0:T(8,128)(2,1)}...) custom-call(bf16[1184,1536]{1,0:T(8,128)(2,1)} %get-tuple-element.36.a_ref,, ...), custom_call_target="tpu_custom_call" | custom-call | tf_op jit(solution)/shard_map/pallas_call | solution.py:602
  323.6 19.2 %shard_map.274 = bf16[1536,6144]{1,0:T(8,128)(2,1)} custom-call(bf16[1184,1536]{1,0:T(8,128)(2,1)} %get-tuple-element.39.refs_0_, bf16[1184,1536]{1,0:T(8,128)(2,1)} %get-tuple-element.40.refs_1_, bf16[1184,1536]{1,0:T(8,128)(2,1)} %get-tuple-element.158.g_hbm.refs_2_, bf16[1184,1536]{1,0:T(8,128)(2,1)} %get-tuple-element.41.refs_3_, f32[12,1536]{1,0:T(8,128)} %copy-done.3), custom_call_target="tpu_custom_call" | custom-call | tf_op jit(solution)/shard_map/pallas_call | solution.py:325
  342.8 110.2 %shard_map.275 = (bf16[1184,1152]{1,0:T(8,128)(2,1)}, bf16[1184,1536]{1,0:T(8,128)(2,1)}) custom-call(bf16[1184,1152]{1,0:T(8,128)(2,1)} %get-tuple-element.37.qkv_ref, bf16[1184,384]{1,0:T(8,128)(2,1)} %get-tuple-element.38.do_ref, bf16[1184,1536]{1,0:T(8,128)(2,1)} %get-tuple-element.43.pm_hbm), custom_call_target="tpu_custom_call" | custom-call | tf_op jit(solution)/shard_map/pallas_call | solution.py:741
  453.1 13.0 %shard_map.276 = bf16[1536,3072]{1,0:T(8,128)(2,1)} custom-call(bf16[1184,1536]{1,0:T(8,128)(2,1)} %get-tuple-element.46.refs_0_, bf16[1184,384]{1,0:T(8,128)(2,1)} %get-tuple-element.47.refs_1_, bf16[1184,1536]{1,0:T(8,128)(2,1)} %copy-done.1, bf16[1184,1152]{1,0:T(8,128)(2,1)} %get-tuple-element.49.refs_3_.x_ref), custom_call_target="tpu_custom_call" | custom-call | tf_op jit(solution)/shard_map/pallas_call | solution.py:325
  468.8 1.5 fusion.30
  472.9 102.4 %shard_map.277 = bf16[1184,1536]{1,0:T(8,128)(2,1)} custom-call(bf16[1184,1152]{1,0:T(8,128)(2,1)S(1)} %copy-done.2, bf16[2,1536,1536]{2,1,0:T(8,128)(2,1)} %all-gather.5.cloned.1.call-done.w_ref.wo_hbm), custom_call_target="tpu_custom_call" | custom-call | tf_op jit(solution)/shard_map/pallas_call | solution.py:401
  576.9 1.6 fusion.32
  578.5 2.5 slice_reduce_fusion
  581.1 3.1 fusion.14
  584.4 11.6 %multiply_reduce_fusion = (bf16[1536]{0:T(1024)(128)(2,1)S(1)}, bf16[1,1024,1536]{2,1,0:T(8,128)(2,1)}, f32[1,1024,1536]{2,1,0:T(8,128)}) fusion(f32[1536]{0:T(1024)S(1)} %get-tuple-element.159, bf16[1184,1536]{1,0:T(8,128)(2,1)} %get-tuple-element.44, bf16[1,1024,1536]{2,1,0:T(8,128)(2,1)S(1)} %copy-done.8, f32[1536]{0:T(1024)S(1)} %get-tuple-element.127, ...), kind=kLoop, calls=%fused_computation.23 | loop fusion | flops 34601472 | bytes 31507456 | tf_op jit(solution)/shard_map/reduce_sum | solution.py:826
  596.1 3.6 multiply_reduce_fusion.1
  600.0 15.5 %all-gather.1 = bf16[8,1,29184]{2,1,0:T(2,128)(2,1)S(1)} all-gather(bf16[1,1,29184]{2,1,0:T(2,128)(2,1)S(1)} %bitcast.93), channel_id=1, replica_groups=mesh['dp'=8,'tensor'=4] {'dp'}, dimensions={0}, use_global_device_ids=true | all-gather | bytes 525312 | tf_op jit(solution)/shard_map/all_gather | solution.py:837
  617.9 2.9 copy.48
  620.8 1.6 reshape.464
  625.6 3.2 copy.47
  628.9 2.2 convolution_bitcast_fusion.2
  631.1 24.5 %all-reduce.2 = f32[8,384]{1,0:T(8,128)S(1)} all-reduce(f32[8,384]{1,0:T(8,128)S(1)} %convolution_bitcast_fusion.2), channel_id=2, replica_groups=mesh['dp'=8,'tensor'=4] {'dp'}, use_global_device_ids=true, to_apply=%region_19.20.clone | all-reduce | flops 3072 | bytes 24576
  661.9 14.2 %reduce-scatter.5.cloned.1.call-done = bf16[192,6144]{1,0:T(8,128)(2,1)} async-done(((bf16[1536,6144]{1,0:T(8,128)(2,1)}), bf16[192,6144]{1,0:T(8,128)(2,1)}) %reduce-scatter.5.cloned.1.call-update) | async-done | bytes 2359312 | tf_op jit(solution)/shard_map/reduce_scatter | solution.py:802
  676.1 2.2 convert_element_type.129
  678.7 1.6 pad_maximum_fusion.3
  680.3 1.6 pad_maximum_fusion.2
  (141 shorter events, 25.6 us)
Async XLA Ops:
  8.0 4.2 copy-start.27
  8.0 15.2 %copy-start.12 = (bf16[2,384,1152]{2,1,0:T(8,128)(2,1)S(1)}, bf16[2,384,1152]{2,1,0:T(8,128)(2,1)}, u32[]{:S(2)}) copy-start(bf16[2,384,1152]{2,1,0:T(8,128)(2,1)} %param.22) | copy-start | bytes 5308420
  8.0 57.5 %all-reduce.5.cloned.1.call-start = ((), (), s32[]{:S(2)}) async-start(), calls=%async_computation.3 | async-start | bytes 147456 | tf_op jit(solution)/shard_map/psum | solution.py:788
  23.3 8.5 %copy-start.18 = (bf16[8,1,384]{2,1,0:T(2,128)(2,1)}, bf16[8,1,384]{2,1,0:T(2,128)(2,1)S(1)}, u32[]{:S(2)}) copy-start(bf16[8,1,384]{2,1,0:T(2,128)(2,1)S(1)} %all-gather) | copy-start | bytes 18436
  31.8 60.9 %all-gather.5.cloned.1.call-start = ((), (), s32[]{:S(2)}) async-start(), calls=%async_computation.4 | async-start | bytes 10616832 | tf_op jit(solution)/shard_map/all_gather | solution.py:771
  32.4 3.7 copy-start.21
  32.4 4.4 copy-start.22
  32.4 5.0 copy-start.23
  32.4 5.6 copy-start.4
  32.4 175.4 %all-gather.7.cloned.1.call-start = ((), (), s32[]{:S(2)}) async-start(), calls=%async_computation.5 | async-start | bytes 21233664 | tf_op jit(solution)/shard_map/all_gather | solution.py:771
  35.9 620.8 %reduce-scatter.3.cloned.1.call-start = ((), (), s32[]{:S(2)}) async-start(), calls=%async_computation.6 | async-start | bytes 10616832 | tf_op jit(solution)/shard_map/reduce_scatter | solution.py:802
  38.0 27.6 %copy-start.20 = (bf16[2,9216]{1,0:T(2,128)(2,1)S(1)}, bf16[2,9216]{1,0:T(2,128)(2,1)}, u32[]{:S(2)}) copy-start(bf16[2,9216]{1,0:T(2,128)(2,1)} %param.23) | copy-start | bytes 110596
  66.5 6.4 copy-start.3
  66.5 2.1 copy-start
  73.0 1.8 copy-start.1
  466.1 0.8 copy-start.24
  466.1 0.8 copy-start.28
  466.1 1.4 copy-start.16
  466.2 4.1 copy-start.5
  466.2 209.9 %reduce-scatter.5.cloned.1.call-start = ((), (), s32[]{:S(2)}) async-start(), calls=%async_computation.7 | async-start | bytes 21233664 | tf_op jit(solution)/shard_map/reduce_scatter | solution.py:802
  467.6 5.3 copy-start.17
  468.8 4.1 copy-start.2
  472.9 104.0 %copy-start.9 = (bf16[1,154,1536]{2,1,0:T(8,128)(2,1)S(1)}, bf16[1,154,1536]{2,1,0:T(8,128)(2,1)}, u32[]{:S(2)}) copy-start(bf16[1,154,1536]{2,1,0:T(8,128)(2,1)} %param.17) | copy-start | bytes 1419268
  575.3 5.8 copy-start.6
  578.5 5.8 copy-start.8
  581.0 3.3 copy-start.7
  584.3 11.7 %copy-start.10 = (bf16[1,154,1536]{2,1,0:T(8,128)(2,1)S(1)}, bf16[1,154,1536]{2,1,0:T(8,128)(2,1)}, u32[]{:S(2)}) copy-start(bf16[1,154,1536]{2,1,0:T(8,128)(2,1)} %param.17) | copy-start | bytes 1419268
  584.3 11.7 %copy-start.13 = (bf16[1,154,1536]{2,1,0:T(8,128)(2,1)S(1)}, bf16[1,154,1536]{2,1,0:T(8,128)(2,1)}, u32[]{:S(2)}) copy-start(bf16[1,154,1536]{2,1,0:T(8,128)(2,1)} %param.21) | copy-start | bytes 1419268
  596.0 21.1 %copy-start.19 = (bf16[8,1,384]{2,1,0:T(2,128)(2,1)S(1)}, bf16[8,1,384]{2,1,0:T(2,128)(2,1)}, u32[]{:S(2)}) copy-start(bf16[8,1,384]{2,1,0:T(2,128)(2,1)} %copy-done.18) | copy-start | bytes 18436
  620.8 34.8 %copy-start.25 = (f32[1,384]{1,0:T(1,128)S(1)}, f32[1,384]{1,0:T(1,128)}, u32[]{:S(2)}) copy-start(f32[1,384]{1,0:T(1,128)} %get-tuple-element.136) | copy-start | bytes 4612
  620.8 34.8 %copy-start.26 = (f32[1,384]{1,0:T(1,128)S(1)}, f32[1,384]{1,0:T(1,128)}, u32[]{:S(2)}) copy-start(f32[1,384]{1,0:T(1,128)} %get-tuple-element.137) | copy-start | bytes 4612
  658.9 1.9 copy-start.11
  (2 other events, 1.4 us)
Sparse Core Ops, SparseCore 0:
  31.9 33.5 all-reduce.4
Sparse Core Ops, SparseCore 1:
  34.8 57.9 all-gather.4
  95.1 98.5 all-gather.6
  466.2 75.7 reduce-scatter.2
  545.6 130.4 reduce-scatter.4
